TPU v7x, 512 devices: a whole 4x8x8 slice. The times are simulated.
512 devices in a mesh: gx: 32 (over x, z), gy: 2 (over y_hi), gz: 8 (over y_lo, core).
Axes of the slice: x: 4, y: 8 (y_hi: 2, y_lo: 4; y = y_hi * 4 + y_lo), z: 8, core: 2. Of those that a mesh axis runs over, the one named last changes fastest.
Arguments:
- coeffs: bfloat16 [16, 1024, 160], P('gz', ('gx', 'gy')), may hold values from -6 to 6
- translations: bfloat16 [16384, 160, 160], P(('gx', 'gz'), 'gy'), may hold values from -0.25 to 0.25
- tmatrix: bfloat16 [1024, 160, 160], P('gx', 'gy'), may hold values from -0.5 to 0.5
- pair_target: int32 [16384], P('gx'), may hold values from 0 to 31
- pair_source: int32 [16384], P('gx'), may hold values from 0 to 1023, as said below
- pair_count: int32 [32], P('gx'), may hold values from 256 to 512, as said below
Outputs:
- result: bfloat16 [16, 1024, 160], P('gz', ('gx', 'gy'))
Inputs may be any that keep to these rules, and one draw needn't show every extreme that they name: `pair_count`: some gx group has all 512 slots live in every draw. The source sphere of a slot of group g lies in group g - 1, g or g + 1 modulo 32, that is pair_source[p] // 32 is one of these.
All inputs are finite; a program needn't handle non-finite values.
Results may differ from a plain program's by a relative error of at most 0.009.
Values may be sent and summed in bfloat16 or wider, within the bound.
A program may use at most 64 MiB of HBM per device.

v0:
```python
import jax
import jax.numpy as jnp
from jax import lax
from jax.sharding import PartitionSpec as P


def padded(value, sides, width):
    for axis, dim in sides:
        devices, length = (lax.axis_size(axis), value.shape[dim])
        up = [(i, (i + 1) % devices) for i in range(devices)]
        down = [(j, i) for i, j in up]
        last = lax.slice_in_dim(value, length - width, length, axis=dim)
        leading = lax.slice_in_dim(value, 0, width, axis=dim)
        before = lax.ppermute(last, axis, up)
        after = lax.ppermute(leading, axis, down)
        value = jnp.concatenate([before, value, after], axis=dim)
    return value


def cut_along(value, dim, devices):
    dims = value.shape
    tiles = value.reshape(*dims[:dim], devices, dims[dim] // devices, *dims[dim + 1 :])
    return jnp.moveaxis(tiles, dim, 0)


def sum_at_owner(value, axis, dim):
    tiles = cut_along(value, dim, lax.axis_size(axis))
    arrived = lax.all_to_all(tiles, axis, split_axis=0, concat_axis=0, tiled=True)
    return arrived.sum(axis=0)


def per_device(coeffs, translations, tmatrix, pair_target, pair_source, pair_count):
    spheres_group = tmatrix.shape[0]
    slots_group = pair_target.shape[0]
    slots_device = translations.shape[0]
    groups_all = lax.axis_size("gx")
    own_group = lax.all_gather(coeffs, "gy", axis=1, tiled=True)
    window = padded(own_group, (("gx", 1),), spheres_group)
    here = lax.axis_index("gx")
    source_group = pair_source // spheres_group
    relative = (source_group - here + 1 + groups_all) % groups_all
    local_index = relative * spheres_group + pair_source % spheres_group
    picked = jnp.take(window, local_index, axis=1)
    living = jnp.arange(slots_group, dtype=jnp.int32) < pair_count[0]
    spheres_here = jnp.arange(spheres_group, dtype=jnp.int32)
    select = ((pair_target[None, :] == spheres_here[:, None]) & living[None, :]).astype(jnp.float32)
    gathered_rhs = lax.all_to_all(picked, "gz", split_axis=1, concat_axis=0, tiled=True)
    contrib = jnp.einsum(
        "pkl,rpl->rpk", translations, gathered_rhs, preferred_element_type=jnp.float32
    )
    own_select = lax.dynamic_slice_in_dim(
        select, lax.axis_index("gz") * slots_device, slots_device, 1
    )
    partial_field = jnp.einsum("sp,rpk->rsk", own_select, contrib)
    near_field = sum_at_owner(partial_field, "gz", 0).astype(jnp.bfloat16)
    scattered = jnp.einsum("rsc,sci->rsi", near_field, tmatrix, preferred_element_type=jnp.float32)
    kept_rows = sum_at_owner(scattered, "gy", 1)
    return (coeffs.astype(jnp.float32) - kept_rows).astype(jnp.bfloat16)


def solution(mesh):
    placed = (
        P("gz", ("gx", "gy"), None),
        P(("gx", "gz"), "gy", None),
        P("gx", "gy", None),
        P("gx"),
        P("gx"),
        P("gx"),
    )
    return jax.shard_map(
        per_device,
        mesh=mesh,
        in_specs=placed,
        out_specs=P("gz", ("gx", "gy"), None),
        check_vma=False,
    )
```

profile of v0, /device:TPU:8, one launch (start us, length us, event | category | flops | bytes accessed | tf_op | source)
XLA Modules:
  0.0 79.1 jit_solution(16993245647487317368)
XLA Ops:
  0.0 0.9 %copy.16 = bf16[2,16,160]{2,0,1:T(2,128)(2,1)S(1)} copy(bf16[2,16,160]{2,1,0:T(8,128)(2,1)} %param.6) | data formatting | bytes 20480 | tf_op args[0]
  0.9 8.3 %all_gather.3 = bf16[2,32,160]{2,0,1:T(2,128)(2,1)S(1)} all-gather(bf16[2,16,160]{2,0,1:T(2,128)(2,1)S(1)} %copy.16), channel_id=1, replica_groups=mesh['gx'=32,'gy'=2,'gz'=8] {'gy'}, dimensions={1}, use_global_device_ids=true | all-gather | bytes 30720 | tf_op jit(solution)/shard_map/all_gather | solution.py:37
  9.2 4.3 %collective-permute-start = (bf16[2,32,160]{2,0,1:T(2,128)(2,1)S(1)}, bf16[2,32,160]{2,0,1:T(2,128)(2,1)S(1)}, u32[]{:S(2)}, u32[]{:S(2)}) collective-permute-start(bf16[2,32,160]{2,0,1:T(2,128)(2,1)S(1)} %all_gather.3), channel_id=1, source_target_pairs={{0,16},{16,32},{32,48},{48,64},{64,80},{80,96},{96,112},{112,128},... | collective-permute-start | bytes 61448 | tf_op jit(solution)/shard_map/ppermute | solution.py:14
  13.5 10.8 %collective-permute-start.1 = (bf16[2,32,160]{2,0,1:T(2,128)(2,1)S(1)}, bf16[2,32,160]{2,0,1:T(2,128)(2,1)S(1)}, u32[]{:S(2)}, u32[]{:S(2)}) collective-permute-start(bf16[2,32,160]{2,0,1:T(2,128)(2,1)S(1)} %all_gather.3), channel_id=1, source_target_pairs={{16,0},{32,16},{48,32},{64,48},{80,64},{96,80},{112,96},{128,112},... | collective-permute-start | bytes 61448 | tf_op jit(solution)/shard_map/ppermute | solution.py:15
  24.3 0.7 compare_and_fusion
  25.0 0.0 collective-permute-done
  25.0 0.8 %collective-permute-done.1 = bf16[2,32,160]{2,0,1:T(2,128)(2,1)S(1)} collective-permute-done((bf16[2,32,160]{2,0,1:T(2,128)(2,1)S(1)}, bf16[2,32,160]{2,0,1:T(2,128)(2,1)S(1)}, u32[]{:S(2)}, u32[]{:S(2)}) %collective-permute-start.1) | collective-permute-done | bytes 20512 | tf_op jit(solution)/shard_map/ppermute | solution.py:15
  25.8 0.2 pad_maximum_fusion
  26.0 2.6 %gather_fusion = bf16[512,2,160]{2,1,0:T(2,128)(2,1)S(1)} fusion(bf16[2,96,160]{2,0,1:T(2,128)(2,1)S(1)} %pad_maximum_fusion, s32[1024]{0:T(1024)S(1)} %pad_clamp_fusion), kind=kCustom, calls=%fused_computation | custom fusion | bytes 657408 | tf_op jit(solution)/shard_map/jit(_take)/gather | solution.py:43
  28.6 2.5 %fusion.3 = bf16[2,512,160]{2,0,1:T(2,128)(2,1)} fusion(bf16[512,2,160]{2,1,0:T(2,128)(2,1)S(1)} %gather_fusion, pred[512]{0:T(512)(128)(4,1)S(1)} %get-tuple-element.5), kind=kLoop, calls=%fused_computation.6 | loop fusion | flops 163840 | bytes 655872 | tf_op jit(solution)/shard_map/jit(_take)/select_n | solution.py:43
  31.1 5.3 %all-to-all-start = ((bf16[2,512,160]{2,0,1:T(2,128)(2,1)}), bf16[2,512,160]{2,0,1:T(2,128)(2,1)S(1)}, u32[]{:S(2)}, u32[]{:S(2)}) async-start(bf16[2,512,160]{2,0,1:T(2,128)(2,1)} %fusion.3), calls=%async_computation | async-start | bytes 1048576 | tf_op jit(solution)/shard_map/all_to_all | solution.py:47
  37.1 0.1 dynamic-slice.1
  37.1 0.8 dynamic-slice
  37.9 10.6 %all-to-all-done = bf16[2,512,160]{2,0,1:T(2,128)(2,1)S(1)} async-done(((bf16[2,512,160]{2,0,1:T(2,128)(2,1)}), bf16[2,512,160]{2,0,1:T(2,128)(2,1)S(1)}, u32[]{:S(2)}, u32[]{:S(2)}) %all-to-all-start) | async-done | bytes 327712 | tf_op jit(solution)/shard_map/all_to_all | solution.py:47
  48.5 0.1 copy.17
  48.6 0.0 copy-done
  48.6 0.0 copy-start.1
  48.6 0.8 %convolution_bitcast_fusion = bf16[16,64,80]{2,0,1:T(8,128)(2,1)S(1)} fusion(bf16[64,80,160]{2,1,0:T(8,128)(2,1)S(1)} %copy-done, bf16[16,64,160]{2,1,0:T(8,128)(2,1)S(1)} %bitcast.24), kind=kOutput, calls=%fused_computation.1 | convolution fusion | flops 26214400 | bytes 2129920 | tf_op jit(solution)/shard_map/pkl,rpl->rpk/dot_general | solution.py:48
  49.4 0.2 fusion
  49.6 13.4 %all_to_all.28 = f32[8,2,32,80]{3,2,1,0:T(8,128)S(1)} all-to-all(f32[8,2,32,80]{3,2,1,0:T(8,128)S(1)} %bitcast.25), channel_id=1, replica_groups=mesh['gx'=32,'gy'=2,'gz'=8] {'gz'}, dimensions={0} | all-to-all | bytes 327680 | tf_op jit(solution)/shard_map/all_to_all | solution.py:28
  63.0 1.6 %fusion.5 = f32[32,2,160]{2,1,0:T(2,128)S(1)} fusion(bf16[32,80,160]{2,1,0:T(8,128)(2,1)} %param.8, bf16[2,32,80]{2,1,0:T(8,128)(2,1)S(1)} %reduce_sum.18), kind=kOutput, calls=%fused_computation.11 | convolution fusion | flops 1638400 | bytes 870400 | tf_op jit(solution)/shard_map/rsc,sci->rsi/dot_general | solution.py:56
  64.6 13.8 %all_to_all.29 = f32[2,2,16,160]{3,1,2,0:T(2,128)S(1)} all-to-all(f32[2,2,16,160]{3,1,2,0:T(2,128)S(1)} %bitcast.26), channel_id=1, replica_groups=mesh['gx'=32,'gy'=2,'gz'=8] {'gy'}, dimensions={0} | all-to-all | bytes 81920 | tf_op jit(solution)/shard_map/all_to_all | solution.py:28
  78.5 0.0 copy-done.1
  78.5 0.6 fusion.4
  (5 shorter events, 0.1 us)
Async XLA Ops:
  0.0 48.6 %copy-start = (bf16[64,80,160]{2,1,0:T(8,128)(2,1)S(1)}, bf16[64,80,160]{2,1,0:T(8,128)(2,1)}, u32[]{:S(2)}) copy-start(bf16[64,80,160]{2,1,0:T(8,128)(2,1)} %param.7) | copy-start | bytes 4915204
  9.2 15.8 %collective-permute-start = (bf16[2,32,160]{2,0,1:T(2,128)(2,1)S(1)}, bf16[2,32,160]{2,0,1:T(2,128)(2,1)S(1)}, u32[]{:S(2)}, u32[]{:S(2)}) collective-permute-start(bf16[2,32,160]{2,0,1:T(2,128)(2,1)S(1)} %all_gather.3), channel_id=1, source_target_pairs={{0,16},{16,32},{32,48},{48,64},{64,80},{80,96},{96,112},{112,128},... | collective-permute-start | bytes 61448 | tf_op jit(solution)/shard_map/ppermute | solution.py:14
  13.5 12.4 %collective-permute-start.1 = (bf16[2,32,160]{2,0,1:T(2,128)(2,1)S(1)}, bf16[2,32,160]{2,0,1:T(2,128)(2,1)S(1)}, u32[]{:S(2)}, u32[]{:S(2)}) collective-permute-start(bf16[2,32,160]{2,0,1:T(2,128)(2,1)S(1)} %all_gather.3), channel_id=1, source_target_pairs={{16,0},{32,16},{48,32},{64,48},{80,64},{96,80},{112,96},{128,112},... | collective-permute-start | bytes 61448 | tf_op jit(solution)/shard_map/ppermute | solution.py:15
  31.1 17.4 %all-to-all-start = ((bf16[2,512,160]{2,0,1:T(2,128)(2,1)}), bf16[2,512,160]{2,0,1:T(2,128)(2,1)S(1)}, u32[]{:S(2)}, u32[]{:S(2)}) async-start(bf16[2,512,160]{2,0,1:T(2,128)(2,1)} %fusion.3), calls=%async_computation | async-start | bytes 1048576 | tf_op jit(solution)/shard_map/all_to_all | solution.py:47
  48.6 29.9 %copy-start.1 = (bf16[2,16,160]{2,1,0:T(8,128)(2,1)S(1)}, bf16[2,16,160]{2,1,0:T(8,128)(2,1)}, u32[]{:S(2)}) copy-start(bf16[2,16,160]{2,1,0:T(8,128)(2,1)} %param.6) | copy-start | bytes 30724
where the time goes:
time: 79.7 us; the launch traced here: 79.1 us
  blocking collectives  35.5 us (45%)
  starting transfers between devices  20.4 us (26%)
  waiting for transfers between devices  11.5 us (14%)
  local copies, waits for them, and re-layouts  4.37 us (5%)
  other arithmetic  4.05 us (5%)
  matrix products  2.6 us (3%)
    all_to_all x2, blocking collectives, sum_at_owner(): lax.all_to_all(tiles, axis, split_axis=0, concat_axis=0, tiled=True)  27.2 us
    ppermute x1, starting transfers between devices, padded(): after = lax.ppermute(leading, axis, down)  10.8 us
    all_to_all x1, waiting for transfers between devices, per_device(): lax.all_to_all(picked, 'gz', split_axis=1, concat_axis=0, tiled=True)  10.6 us
    all_gather x1, blocking collectives, per_device(): own_group = lax.all_gather(coeffs, 'gy', axis=1, tiled=True)  8.31 us
    all_to_all x1, starting transfers between devices, per_device(): lax.all_to_all(picked, 'gz', split_axis=1, concat_axis=0, tiled=True)  5.32 us
    ppermute x1, starting transfers between devices, padded(): before = lax.ppermute(last, axis, up)  4.27 us
    gather x1, local copies, waits for them, and re-layouts, per_device(): picked = jnp.take(window, local_index, axis=1)  2.57 us
    select_n x1, other arithmetic, per_device(): picked = jnp.take(window, local_index, axis=1)  2.5 us
  transfers between devices with their start and end apart: 3, of which 2 were waited for; matrix products, arithmetic and copies ran while one was open for 2% of the time, Pallas kernels for 0%

commit v1 on v0

v1 whole, which is shorter than its diff:
```python
import functools

import jax
import jax.numpy as jnp
from jax import lax
from jax.experimental import pallas as pl
from jax.experimental.pallas import tpu as pltpu
from jax.sharding import PartitionSpec as P

MESH = pl.DeviceIdType.MESH
F32 = jnp.float32
BF16 = jnp.bfloat16
NT = (((1,), (1,)), ((), ()))
RING = 8
NEAR_FIRST = (1, 7, 2, 6, 3, 5, 4)
FAR_FIRST = (4, 3, 5, 2, 6, 1, 7)


def packed_rows(rows):
    tails = [rows[8 * j : 8 * j + 8, 128:160] for j in range(4)]
    tail = jnp.concatenate(tails, axis=1)
    return jnp.concatenate([rows[:, :128], tail, jnp.zeros_like(tail)], axis=0)


def tail_rows(tail):
    return jnp.concatenate([tail[:, 32 * j : 32 * j + 32] for j in range(4)], axis=0)


def kernel(
    groups, count, target, source, coeffs_hbm, trans_hbm, tmat_hbm, out,
    coeffs, trans, tmat, win, tails, pick, place, picked, contrib, near, scat, parts, sums,
    local_sem, send_y, send_z, recv, pair_send, pair_recv, send_out, recv_out,
):
    gx, gy, gz = lax.axis_index("gx"), lax.axis_index("gy"), lax.axis_index("gz")
    quarter, core = gz // 2, gz % 2
    here = gy * 4 + quarter
    half = trans_hbm.shape[0]
    pairs = 2 * half

    def at(y):
        return {"gx": gx, "gy": y // 4, "gz": (y % 4) * 2 + core}

    up = {"gx": (gx + 1) % groups, "gy": gy, "gz": gz}
    down = {"gx": (gx + groups - 1) % groups, "gy": gy, "gz": gz}
    sibling = {"gx": gx, "gy": gy, "gz": quarter * 2 + 1 - core}

    load_c = pltpu.make_async_copy(coeffs_hbm, coeffs, local_sem.at[0])
    load_t = pltpu.make_async_copy(trans_hbm, trans.at[pl.ds(core * half, half)], local_sem.at[1])
    load_m = pltpu.make_async_copy(tmat_hbm, tmat, local_sem.at[2])
    load_c.start()
    load_t.start()
    load_m.start()

    barrier = pltpu.get_barrier_semaphore()
    for d in FAR_FIRST:
        pl.semaphore_signal(barrier, inc=1, device_id=at((here + d) % RING), device_id_type=MESH)
    for peer in (up, down, sibling):
        pl.semaphore_signal(barrier, inc=1, device_id=peer, device_id_type=MESH)

    load_c.wait()
    own = coeffs[...].astype(F32).reshape(32, 160)
    win[RING + here] = packed_rows(own).astype(BF16)

    lane = lax.broadcasted_iota(jnp.int32, (8, 128), 1)
    sub = lax.broadcasted_iota(jnp.int32, (8, 128), 0)
    diagonal = lane - 16 * sub

    def build_pick(j, carry):
        codes = []
        for u in range(2):
            s = source[quarter * pairs + 2 * j + u]
            relative = (s // 32 - gx + 1 + groups) % groups
            codes.append((relative * 2 + (s % 32) // 16) * 1024 + s % 16)
        for t in range(6):
            hot = [jnp.where(diagonal == c - 1024 * t, 1.0, 0.0) for c in codes]
            pick[pl.ds(pl.multiple_of(16 * j, 16), 16), 128 * t : 128 * t + 128] = jnp.concatenate(hot, axis=0).astype(BF16)
        return carry

    lax.fori_loop(0, pairs // 2, build_pick, 0)

    def build_place(q, carry):
        v = jnp.full((8, 128), -1, jnp.int32)
        for i in range(16):
            slot = quarter * pairs + q * 16 + i
            t = jnp.where(slot < count[0], target[slot], -1)
            v = jnp.where((lane // 8 == i) & (lane % 8 == sub), t, v)
        for s in range(16):
            hot = [jnp.where(v == 2 * s + u, 1.0, 0.0) for u in range(2)]
            place[16 * s : 16 * s + 16, pl.ds(pl.multiple_of(128 * q, 128), 128)] = jnp.concatenate(hot, axis=0).astype(BF16)
        return carry

    lax.fori_loop(0, pairs // 16, build_place, 0)

    load_t.wait()
    pl.semaphore_wait(barrier, 10)

    def remote(src, dst, s, r, peer):
        return pltpu.make_async_remote_copy(
            src_ref=src, dst_ref=dst, send_sem=s, recv_sem=r, device_id=peer, device_id_type=MESH
        )

    sends = []

    def start(copy):
        copy.start()
        sends.append(copy)

    def forward(y):
        block = win.at[RING + y]
        start(remote(block, win.at[y], send_z.at[y], recv.at[y], up))
        start(remote(block, win.at[2 * RING + y], send_z.at[RING + y], recv.at[2 * RING + y], down))

    def unpack(slot):
        tail = tail_rows(win[slot, 32:48, :].astype(F32)[0:8])
        tails[slot] = tail.astype(BF16)

    def arrive(slot):
        remote(win.at[slot], win.at[slot], send_y.at[0], recv.at[slot], sibling).wait_recv()

    for d in FAR_FIRST:
        start(remote(win.at[RING + here], win.at[RING + here], send_y.at[d], recv.at[RING + here], at((here + d) % RING)))
    forward(here)
    mine = trans.at[pl.ds(core * half, half)]
    start(remote(mine, mine, pair_send, pair_recv, sibling))
    unpack(RING + here)
    for d in NEAR_FIRST:
        y = (here + d) % RING
        arrive(RING + y)
        forward(y)
        unpack(RING + y)

    def group_rows(g):
        block = win[8 * g : 8 * g + 8, 0:32, :].reshape(256, 128)
        return jnp.concatenate([block, tails[8 * g : 8 * g + 8].reshape(256, 32)], axis=1)

    def pick_group(g, q):
        rows = pick[pl.ds(pl.multiple_of(128 * q, 128), 128), 256 * g : 256 * g + 256]
        return jnp.dot(rows, group_rows(g), preferred_element_type=F32).astype(BF16)

    def pick_own(q, carry):
        picked[q] = pick_group(1, q)
        return carry

    lax.fori_loop(0, 8, pick_own, 0)

    for d in (0,) + NEAR_FIRST:
        y = (here + d) % RING
        for slot in (y, 2 * RING + y):
            arrive(slot)
            unpack(slot)
    remote(mine, trans.at[pl.ds((1 - core) * half, half)], pair_send, pair_recv, sibling).wait_recv()

    chosen = lax.broadcasted_iota(jnp.int32, (16, 80, 128), 2) // 8 == lax.broadcasted_iota(jnp.int32, (16, 80, 128), 0)

    def translate(q, carry):
        rows = picked[q] + pick_group(0, q) + pick_group(2, q)
        blocks = trans[pl.ds(16 * q, 16)].reshape(1280, 160)
        every = lax.dot_general(blocks, rows, NT, preferred_element_type=F32).reshape(16, 80, 128)
        contrib[:, pl.ds(pl.multiple_of(128 * q, 128), 128)] = jnp.where(chosen, every, 0.0).sum(axis=0).astype(BF16)
        return carry

    lax.fori_loop(0, pairs // 16, translate, 0)

    near[...] = lax.dot_general(place[...], contrib[...], NT, preferred_element_type=F32).astype(BF16)
    load_m.wait()

    def scatter(j, carry):
        rows = near[pl.ds(pl.multiple_of(16 * j, 16), 16), :]
        for u in range(2):
            both = jnp.dot(rows, tmat[2 * j + u], preferred_element_type=F32)
            scat[2 * j + u] = both[8 * u : 8 * u + 8]
        return carry

    lax.fori_loop(0, 16, scatter, 0)

    for y in range(RING):
        h, r = y // 4, 2 * (y % 4)
        rows = jnp.concatenate([scat[16 * h : 16 * h + 16, r + u, :] for u in range(2)], axis=0)
        parts[y] = packed_rows(rows).astype(BF16)
    for d in FAR_FIRST:
        y = (here + d) % RING
        start(remote(parts.at[y], sums.at[here], send_out.at[d], recv_out.at[here], at(y)))
    total = parts[here].astype(F32)
    for d in NEAR_FIRST:
        y = (here + d) % RING
        remote(parts.at[y], sums.at[y], send_out.at[d], recv_out.at[y], sibling).wait_recv()
        total = total + sums[y].astype(F32)
    whole = jnp.concatenate([total[0:32], tail_rows(total[32:40])], axis=1)
    out[...] = (coeffs[...].astype(F32) - whole.reshape(2, 16, 160)).astype(BF16)
    for copy in sends:
        copy.wait_send()


def solution(mesh):
    groups = mesh.shape["gx"]

    def step(coeffs, translations, tmatrix, pair_target, pair_source, pair_count):
        half = translations.shape[0]
        smem = pl.BlockSpec(memory_space=pltpu.SMEM)
        hbm = pl.BlockSpec(memory_space=pl.ANY)
        return pl.pallas_call(
            functools.partial(kernel, groups),
            out_shape=jax.ShapeDtypeStruct(coeffs.shape, BF16),
            in_specs=[smem, smem, smem, hbm, hbm, hbm],
            out_specs=pl.BlockSpec(memory_space=pltpu.VMEM),
            scratch_shapes=[
                pltpu.VMEM(coeffs.shape, BF16),
                pltpu.VMEM((2 * half, 80, 160), BF16),
                pltpu.VMEM((32, 80, 160), BF16),
                pltpu.VMEM((24, 48, 128), BF16),
                pltpu.VMEM((24, 32, 32), BF16),
                pltpu.VMEM((1024, 768), BF16),
                pltpu.VMEM((256, 1024), BF16),
                pltpu.VMEM((8, 128, 160), BF16),
                pltpu.VMEM((80, 1024), BF16),
                pltpu.VMEM((256, 80), BF16),
                pltpu.VMEM((32, 8, 160), F32),
                pltpu.VMEM((8, 48, 128), BF16),
                pltpu.VMEM((8, 48, 128), BF16),
                pltpu.SemaphoreType.DMA((3,)),
                pltpu.SemaphoreType.DMA((8,)),
                pltpu.SemaphoreType.DMA((16,)),
                pltpu.SemaphoreType.DMA((24,)),
                pltpu.SemaphoreType.DMA,
                pltpu.SemaphoreType.DMA,
                pltpu.SemaphoreType.DMA((8,)),
                pltpu.SemaphoreType.DMA((8,)),
            ],
            compiler_params=pltpu.CompilerParams(
                collective_id=0, has_side_effects=True, vmem_limit_bytes=40 << 20
            ),
        )(pair_count, pair_target, pair_source, coeffs, translations, tmatrix)

    placed = (
        P("gz", ("gx", "gy"), None),
        P(("gx", "gz"), "gy", None),
        P("gx", "gy", None),
        P("gx"),
        P("gx"),
        P("gx"),
    )
    return jax.shard_map(
        step, mesh=mesh, in_specs=placed, out_specs=P("gz", ("gx", "gy"), None), check_vma=False
    )
```

time: 79.7 us -> 43.3 us (0.54)
  Pallas kernels: 0 us -> 36.6 us
  blocking collectives: 35.5 us -> 0 us
  starting transfers between devices: 20.4 us -> 0 us
  waiting for transfers between devices: 11.5 us -> 0 us
  other arithmetic: 4.05 us -> 0 us
  matrix products: 2.6 us -> 0 us
  local copies, waits for them, and re-layouts: 4.37 us -> 5.74 us
    pallas_call x0 -> x1, Pallas kernels: none -> 36.6 us  [step(): pl.pallas_call(functools.partial(kernel, groups), out_shape=jax.ShapeDtyp...]
    all_to_all x2 -> x0, blocking collectives: 27.2 us -> none  [sum_at_owner(): lax.all_to_all(tiles, axis, split_axis=0, concat_axis=0, tiled=True)]
    ppermute x2 -> x0, starting transfers between devices: 15.1 us -> none  [the longest x1 10.8 us: padded(): after = lax.ppermute(leading, axis, down)]
    all_to_all x1 -> x0, waiting for transfers between devices: 10.6 us -> none  [per_device(): lax.all_to_all(picked, 'gz', split_axis=1, concat_axis=0, tiled=True)]
    all_gather x1 -> x0, blocking collectives: 8.31 us -> none  [per_device(): own_group = lax.all_gather(coeffs, 'gy', axis=1, tiled=True)]
    all_to_all x1 -> x0, starting transfers between devices: 5.32 us -> none  [per_device(): lax.all_to_all(picked, 'gz', split_axis=1, concat_axis=0, tiled=True)]
    unnamed x5 -> x11, local copies, waits for them, and re-layouts: 0.89 us -> 5.74 us
    dot_general x3 -> x0, matrix products: 2.6 us -> none  [the longest x1 1.59 us: per_device(): jnp.einsum('rsc,sci->rsi', near_field, tmatrix, preferred_element_type=jn...]
  transfers between devices with their start and end apart: 3 -> 0, of which waited for: 2 -> 0; matrix products, arithmetic and copies ran while one was open for 2% -> 0% of each run, Pallas kernels for 0% -> 0%
where the time goes in v1:
time: 43.3 us; the launch traced here: 43 us
  Pallas kernels  36.6 us (85%)
  local copies, waits for them, and re-layouts  5.74 us (13%)
  between operations  0.67 us (2%)
    pallas_call x1, Pallas kernels, step(): pl.pallas_call(functools.partial(kernel, groups), out_shape=jax.ShapeDtyp...  36.6 us
    unnamed x11, local copies, waits for them, and re-layouts  5.74 us

profile of v1, /device:TPU:8, one launch (start us, length us, event | category | flops | bytes accessed | tf_op | source)
XLA Modules:
  0.0 43.0 jit_solution(3969301282242289191)
XLA Ops:
  0.7 0.0 copy-start
  0.7 1.7 %copy-done = bf16[64,80,160]{2,1,0:T(8,128)(2,1)S(1)} copy-done((bf16[64,80,160]{2,1,0:T(8,128)(2,1)S(1)}, bf16[64,80,160]{2,1,0:T(8,128)(2,1)}, u32[]{:S(2)}) %copy-start) | copy-done | bytes 1638424
  2.4 0.0 copy-start.1
  2.4 1.3 %copy-done.1 = bf16[32,80,160]{2,1,0:T(8,128)(2,1)S(1)} copy-done((bf16[32,80,160]{2,1,0:T(8,128)(2,1)S(1)}, bf16[32,80,160]{2,1,0:T(8,128)(2,1)}, u32[]{:S(2)}) %copy-start.1) | copy-done | bytes 819224
  3.7 0.0 copy-start.2
  3.7 0.7 %copy-done.2 = bf16[2,16,160]{2,1,0:T(8,128)(2,1)S(1)} copy-done((bf16[2,16,160]{2,1,0:T(8,128)(2,1)S(1)}, bf16[2,16,160]{2,1,0:T(8,128)(2,1)}, u32[]{:S(2)}) %copy-start.2) | copy-done | bytes 10264
  4.4 0.0 copy-start.3
  4.4 0.7 %copy-done.3 = s32[512]{0:T(512)S(1)} copy-done((s32[512]{0:T(512)S(1)}, s32[512]{0:T(512)}, u32[]{:S(2)}) %copy-start.3) | copy-done | bytes 2072
  5.1 0.0 copy-start.4
  5.1 0.7 %copy-done.4 = s32[512]{0:T(512)S(1)} copy-done((s32[512]{0:T(512)S(1)}, s32[512]{0:T(512)}, u32[]{:S(2)}) %copy-start.4) | copy-done | bytes 2072
  5.8 36.6 %shard_map.64 = bf16[2,16,160]{2,1,0:T(8,128)(2,1)S(1)} custom-call(s32[1]{0:T(128)S(6)} %copy.8.count, s32[512]{0:T(512)S(1)} %copy-done.3, s32[512]{0:T(512)S(1)} %copy-done.4, bf16[2,16,160]{2,1,0:T(8,128)(2,1)S(1)} %copy-done.2, bf16[64,80,160]{2,1,0:T(8,128)(2,1)S(1)} %copy-done, bf16[32,80,160]{2,1,0:T(8,128)(2,1)S(1)} %copy-done.1), custom_call_target="tpu_custom_call" | custom-call | tf_op jit(solution)/shard_map/pallas_call | solution.py:201
  42.4 0.6 %copy.9 = bf16[2,16,160]{2,1,0:T(8,128)(2,1)} copy(bf16[2,16,160]{2,1,0:T(8,128)(2,1)S(1)} %shard_map.64) | data formatting | bytes 20480
Async XLA Ops:
  0.7 1.7 %copy-start = (bf16[64,80,160]{2,1,0:T(8,128)(2,1)S(1)}, bf16[64,80,160]{2,1,0:T(8,128)(2,1)}, u32[]{:S(2)}) copy-start(bf16[64,80,160]{2,1,0:T(8,128)(2,1)} %trans_hbm.1) | copy-start | bytes 4915204
  2.4 1.3 %copy-start.1 = (bf16[32,80,160]{2,1,0:T(8,128)(2,1)S(1)}, bf16[32,80,160]{2,1,0:T(8,128)(2,1)}, u32[]{:S(2)}) copy-start(bf16[32,80,160]{2,1,0:T(8,128)(2,1)} %tmat_hbm.1) | copy-start | bytes 2457604
  3.7 0.7 %copy-start.2 = (bf16[2,16,160]{2,1,0:T(8,128)(2,1)S(1)}, bf16[2,16,160]{2,1,0:T(8,128)(2,1)}, u32[]{:S(2)}) copy-start(bf16[2,16,160]{2,1,0:T(8,128)(2,1)} %coeffs_hbm.1) | copy-start | bytes 30724
  4.4 0.7 %copy-start.3 = (s32[512]{0:T(512)S(1)}, s32[512]{0:T(512)}, u32[]{:S(2)}) copy-start(s32[512]{0:T(512)} %target.1) | copy-start | bytes 6148
  5.1 0.7 %copy-start.4 = (s32[512]{0:T(512)S(1)}, s32[512]{0:T(512)}, u32[]{:S(2)}) copy-start(s32[512]{0:T(512)} %source.1) | copy-start | bytes 6148

commit v2 on v1

--- a/solution.py
+++ b/solution.py
@@ -27,8 +27,8 @@
 
 
 def kernel(
-    groups, count, target, source, coeffs_hbm, trans_hbm, tmat_hbm, out,
-    coeffs, trans, tmat, win, tails, pick, place, picked, contrib, near, scat, parts, sums,
+    groups, count_hbm, target_hbm, source_hbm, coeffs_hbm, trans_hbm, tmat_hbm, out,
+    count, target, source, coeffs, trans, tmat, win, tails, pick, place, picked, contrib, near, scat, parts, sums,
     local_sem, send_y, send_z, recv, pair_send, pair_recv, send_out, recv_out,
 ):
     gx, gy, gz = lax.axis_index("gx"), lax.axis_index("gy"), lax.axis_index("gz")
@@ -47,7 +47,14 @@
     load_c = pltpu.make_async_copy(coeffs_hbm, coeffs, local_sem.at[0])
     load_t = pltpu.make_async_copy(trans_hbm, trans.at[pl.ds(core * half, half)], local_sem.at[1])
     load_m = pltpu.make_async_copy(tmat_hbm, tmat, local_sem.at[2])
+    load_p = [
+        pltpu.make_async_copy(count_hbm, count, local_sem.at[3]),
+        pltpu.make_async_copy(target_hbm, target, local_sem.at[4]),
+        pltpu.make_async_copy(source_hbm, source, local_sem.at[5]),
+    ]
     load_c.start()
+    for load in load_p:
+        load.start()
     load_t.start()
     load_m.start()
 
@@ -61,6 +68,8 @@
     own = coeffs[...].astype(F32).reshape(32, 160)
     win[RING + here] = packed_rows(own).astype(BF16)
 
+    for load in load_p:
+        load.wait()
     lane = lax.broadcasted_iota(jnp.int32, (8, 128), 1)
     sub = lax.broadcasted_iota(jnp.int32, (8, 128), 0)
     diagonal = lane - 16 * sub
@@ -196,14 +205,16 @@
 
     def step(coeffs, translations, tmatrix, pair_target, pair_source, pair_count):
         half = translations.shape[0]
-        smem = pl.BlockSpec(memory_space=pltpu.SMEM)
-        hbm = pl.BlockSpec(memory_space=pl.ANY)
+        hbm = pl.BlockSpec(memory_space=pltpu.HBM)
         return pl.pallas_call(
             functools.partial(kernel, groups),
             out_shape=jax.ShapeDtypeStruct(coeffs.shape, BF16),
-            in_specs=[smem, smem, smem, hbm, hbm, hbm],
+            in_specs=[hbm] * 6,
             out_specs=pl.BlockSpec(memory_space=pltpu.VMEM),
             scratch_shapes=[
+                pltpu.SMEM(pair_count.shape, jnp.int32),
+                pltpu.SMEM(pair_target.shape, jnp.int32),
+                pltpu.SMEM(pair_source.shape, jnp.int32),
                 pltpu.VMEM(coeffs.shape, BF16),
                 pltpu.VMEM((2 * half, 80, 160), BF16),
                 pltpu.VMEM((32, 80, 160), BF16),
@@ -217,7 +228,7 @@
                 pltpu.VMEM((32, 8, 160), F32),
                 pltpu.VMEM((8, 48, 128), BF16),
                 pltpu.VMEM((8, 48, 128), BF16),
-                pltpu.SemaphoreType.DMA((3,)),
+                pltpu.SemaphoreType.DMA((6,)),
                 pltpu.SemaphoreType.DMA((8,)),
                 pltpu.SemaphoreType.DMA((16,)),
                 pltpu.SemaphoreType.DMA((24,)),
@@ -227,7 +238,7 @@
                 pltpu.SemaphoreType.DMA((8,)),
             ],
             compiler_params=pltpu.CompilerParams(
-                collective_id=0, has_side_effects=True, vmem_limit_bytes=40 << 20
+                collective_id=0, has_side_effects=True, vmem_limit_bytes=67_043_328
             ),
         )(pair_count, pair_target, pair_source, coeffs, translations, tmatrix)
 

time: 43.3 us -> 39.4 us (0.910)
  local copies, waits for them, and re-layouts: 5.74 us -> 1.32 us
  Pallas kernels: 36.6 us -> 37.1 us
    unnamed x11 -> x1, local copies, waits for them, and re-layouts: 5.74 us -> 1.32 us
    pallas_call x1, Pallas kernels: 36.6 us -> 37.1 us  [step(): pl.pallas_call(functools.partial(kernel, groups), out_shape=jax.ShapeDtyp...]
where the time goes in v2:
time: 39.4 us; the launch traced here: 39.1 us
  Pallas kernels  37.1 us (94%)
  local copies, waits for them, and re-layouts  1.32 us (3%)
  between operations  0.66 us (2%)
    pallas_call x1, Pallas kernels, step(): pl.pallas_call(functools.partial(kernel, groups), out_shape=jax.ShapeDtyp...  37.1 us
    unnamed x1, local copies, waits for them, and re-layouts  1.32 us

profile of v2, /device:TPU:8, one launch (start us, length us, event | category | flops | bytes accessed | tf_op | source)
XLA Modules:
  0.0 39.1 jit_solution(9615075988250383596)
XLA Ops:
  0.7 37.1 %shard_map.64 = bf16[2,16,160]{2,1,0:T(8,128)(2,1)} custom-call(s32[1]{0:T(128)S(6)} %copy.8.count_hbm, s32[512]{0:T(512)} %target_hbm.1, s32[512]{0:T(512)} %source_hbm.1, bf16[2,16,160]{2,1,0:T(8,128)(2,1)} %coeffs_hbm.1, bf16[64,80,160]{2,1,0:T(8,128)(2,1)} %trans_hbm.1, bf16[32,80,160]{2,1,0:T(8,128)(2,1)} %tmat_hbm.1), custom_call_target="tpu_custom_call" | custom-call | tf_op jit(solution)/shard_map/pallas_call | solution.py:209
  37.8 1.3 %copy.9 = bf16[2,16,160]{2,1,0:T(8,128)(2,1)} copy(bf16[2,16,160]{2,1,0:T(8,128)(2,1)} %shard_map.64) | data formatting | bytes 20480

commit v3 on v1

v3 whole, which is shorter than its diff:
```python
import functools

import jax
import jax.numpy as jnp
from jax import lax
from jax.experimental import pallas as pl
from jax.experimental.pallas import tpu as pltpu
from jax.sharding import PartitionSpec as P

MESH = pl.DeviceIdType.MESH
F32 = jnp.float32
BF16 = jnp.bfloat16
NT = (((1,), (1,)), ((), ()))
RING = 8
NEAR_FIRST = (1, 7, 2, 6, 3, 5, 4)
FAR_FIRST = (4, 3, 5, 2, 6, 1, 7)


def packed_rows(rows):
    tails = [rows[8 * j : 8 * j + 8, 128:160] for j in range(4)]
    tail = jnp.concatenate(tails, axis=1)
    return jnp.concatenate([rows[:, :128], tail, jnp.zeros_like(tail)], axis=0)


def tail_rows(tail):
    return jnp.concatenate([tail[:, 32 * j : 32 * j + 32] for j in range(4)], axis=0)


def kernel(
    groups, count, target_hbm, source_hbm, coeffs_hbm, trans_hbm, tmat_hbm, out,
    target, source, coeffs, trans, tmat, win, tails, pick, place, picked, contrib, near, scat, parts, sums,
    local_sem, send_y, send_z, recv, pair_send, pair_recv, send_out, recv_out,
):
    load_c = pltpu.make_async_copy(coeffs_hbm, coeffs, local_sem.at[0])
    load_c.start()

    gx, gy, gz = lax.axis_index("gx"), lax.axis_index("gy"), lax.axis_index("gz")
    quarter, core = gz // 2, gz % 2
    here = gy * 4 + quarter
    half = trans_hbm.shape[0]
    pairs = 2 * half

    def at(y):
        return {"gx": gx, "gy": y // 4, "gz": (y % 4) * 2 + core}

    up = {"gx": (gx + 1) % groups, "gy": gy, "gz": gz}
    down = {"gx": (gx + groups - 1) % groups, "gy": gy, "gz": gz}
    sibling = {"gx": gx, "gy": gy, "gz": quarter * 2 + 1 - core}
    ring = [(here + d) % RING for d in range(RING)]

    barrier = pltpu.get_barrier_semaphore()
    for d in FAR_FIRST:
        pl.semaphore_signal(barrier, inc=1, device_id=at(ring[d]), device_id_type=MESH)
    for peer in (up, down, sibling):
        pl.semaphore_signal(barrier, inc=1, device_id=peer, device_id_type=MESH)

    load_p = [
        pltpu.make_async_copy(target_hbm, target, local_sem.at[3]),
        pltpu.make_async_copy(source_hbm, source, local_sem.at[4]),
    ]
    load_t = pltpu.make_async_copy(trans_hbm, trans.at[pl.ds(core * half, half)], local_sem.at[1])
    load_m = pltpu.make_async_copy(tmat_hbm, tmat, local_sem.at[2])
    for load in load_p:
        load.start()
    load_t.start()
    load_m.start()

    load_c.wait()
    own = coeffs[...].astype(F32).reshape(32, 160)
    win[RING + here] = packed_rows(own).astype(BF16)

    pl.semaphore_wait(barrier, 10)

    def remote(src, dst, s, r, peer):
        return pltpu.make_async_remote_copy(
            src_ref=src, dst_ref=dst, send_sem=s, recv_sem=r, device_id=peer, device_id_type=MESH
        )

    sends = []

    def start(copy):
        copy.start()
        sends.append(copy)

    def forward(y):
        block = win.at[RING + y]
        start(remote(block, win.at[y], send_z.at[y], recv.at[y], up))
        start(remote(block, win.at[2 * RING + y], send_z.at[RING + y], recv.at[2 * RING + y], down))

    def unpack(slot):
        tail = tail_rows(win[slot, 32:48, :].astype(F32)[0:8])
        tails[slot] = tail.astype(BF16)

    def arrive(slot):
        remote(win.at[slot], win.at[slot], send_y.at[0], recv.at[slot], sibling).wait_recv()

    for d in FAR_FIRST:
        start(remote(win.at[RING + here], win.at[RING + here], send_y.at[d], recv.at[RING + here], at(ring[d])))
    forward(here)
    load_t.wait()
    mine = trans.at[pl.ds(core * half, half)]
    start(remote(mine, mine, pair_send, pair_recv, sibling))

    for load in load_p:
        load.wait()
    lane = lax.broadcasted_iota(jnp.int32, (8, 128), 1)
    sub = lax.broadcasted_iota(jnp.int32, (8, 128), 0)
    diagonal = lane - 16 * sub

    def build_pick(j, carry):
        for v in range(4):
            codes = []
            for u in range(2):
                s = source[quarter * pairs + 8 * j + 2 * v + u]
                relative = (s // 32 - gx + 1 + groups) % groups
                codes.append((relative * 2 + (s % 32) // 16) * 1024 + s % 16)
            rows = pl.ds(pl.multiple_of(64 * j + 16 * v, 16), 16)
            for t in range(6):
                hot = [jnp.where(diagonal == c - 1024 * t, 1.0, 0.0) for c in codes]
                pick[rows, 128 * t : 128 * t + 128] = jnp.concatenate(hot, axis=0).astype(BF16)
        return carry

    lax.fori_loop(0, pairs // 8, build_pick, 0)

    for d in NEAR_FIRST:
        arrive(RING + ring[d])
        forward(ring[d])

    def build_place(q, carry):
        v = jnp.full((8, 128), -1, jnp.int32)
        for i in range(16):
            slot = quarter * pairs + q * 16 + i
            t = jnp.where(slot < count[0], target[slot], -1)
            v = jnp.where((lane // 8 == i) & (lane % 8 == sub), t, v)
        for s in range(16):
            hot = [jnp.where(v == 2 * s + u, 1.0, 0.0) for u in range(2)]
            place[16 * s : 16 * s + 16, pl.ds(pl.multiple_of(128 * q, 128), 128)] = jnp.concatenate(hot, axis=0).astype(BF16)
        return carry

    lax.fori_loop(0, pairs // 16, build_place, 0)

    def group_rows(g):
        for y in range(RING):
            unpack(RING * g + y)
        block = win[8 * g : 8 * g + 8, 0:32, :].reshape(256, 128)
        return jnp.concatenate([block, tails[8 * g : 8 * g + 8].reshape(256, 32)], axis=1)

    rows = group_rows(1)
    for q in range(4):
        chunk = jnp.dot(pick[256 * q : 256 * q + 256, 256:512], rows, preferred_element_type=F32)
        picked[256 * q : 256 * q + 256] = chunk.astype(BF16)

    for d in (0,) + NEAR_FIRST:
        arrive(ring[d])
        arrive(2 * RING + ring[d])
    rows = [group_rows(0), group_rows(2)]
    for q in range(4):
        part = pl.ds(256 * q, 256)
        chunk = [
            jnp.dot(pick[part, 512 * u : 512 * u + 256], rows[u], preferred_element_type=F32).astype(BF16)
            for u in range(2)
        ]
        picked[part] = picked[part] + chunk[0] + chunk[1]
    remote(mine, trans.at[pl.ds((1 - core) * half, half)], pair_send, pair_recv, sibling).wait_recv()

    chosen = lax.broadcasted_iota(jnp.int32, (16, 80, 128), 2) // 8 == lax.broadcasted_iota(jnp.int32, (16, 80, 128), 0)
    for q in range(8):
        blocks = trans[16 * q : 16 * q + 16].reshape(1280, 160)
        every = lax.dot_general(blocks, picked[128 * q : 128 * q + 128], NT, preferred_element_type=F32)
        every = jnp.where(chosen, every.reshape(16, 80, 128), 0.0).sum(axis=0)
        contrib[:, 128 * q : 128 * q + 128] = every.astype(BF16)

    near[...] = lax.dot_general(place[...], contrib[...], NT, preferred_element_type=F32).astype(BF16)
    load_m.wait()

    for j in range(16):
        rows = near[16 * j : 16 * j + 16, :]
        for u in range(2):
            both = jnp.dot(rows, tmat[2 * j + u], preferred_element_type=F32)
            scat[2 * j + u] = both[8 * u : 8 * u + 8]

    for y in range(RING):
        h, r = y // 4, 2 * (y % 4)
        rows = jnp.concatenate([scat[16 * h : 16 * h + 16, r + u, :] for u in range(2)], axis=0)
        parts[y] = packed_rows(rows).astype(BF16)
    for d in FAR_FIRST:
        start(remote(parts.at[ring[d]], sums.at[here], send_out.at[d], recv_out.at[here], at(ring[d])))
    total = parts[here].astype(F32)
    for d in NEAR_FIRST:
        y = ring[d]
        remote(parts.at[y], sums.at[y], send_out.at[d], recv_out.at[y], sibling).wait_recv()
        total = total + sums[y].astype(F32)
    whole = jnp.concatenate([total[0:32], tail_rows(total[32:40])], axis=1)
    out[...] = (coeffs[...].astype(F32) - whole.reshape(2, 16, 160)).astype(BF16)
    for copy in sends:
        copy.wait_send()


def solution(mesh):
    groups = mesh.shape["gx"]

    def step(coeffs, translations, tmatrix, pair_target, pair_source, pair_count):
        half = translations.shape[0]
        hbm = pl.BlockSpec(memory_space=pltpu.HBM)
        return pl.pallas_call(
            functools.partial(kernel, groups),
            out_shape=pltpu.VMEM(coeffs.shape, BF16),
            in_specs=[pl.BlockSpec(memory_space=pltpu.SMEM)] + [hbm] * 5,
            out_specs=pl.BlockSpec(memory_space=pltpu.VMEM),
            scratch_shapes=[
                pltpu.SMEM(pair_target.shape, jnp.int32),
                pltpu.SMEM(pair_source.shape, jnp.int32),
                pltpu.VMEM(coeffs.shape, BF16),
                pltpu.VMEM((2 * half, 80, 160), BF16),
                pltpu.VMEM((32, 80, 160), BF16),
                pltpu.VMEM((24, 48, 128), BF16),
                pltpu.VMEM((24, 32, 32), BF16),
                pltpu.VMEM((1024, 768), BF16),
                pltpu.VMEM((256, 1024), BF16),
                pltpu.VMEM((1024, 160), BF16),
                pltpu.VMEM((80, 1024), BF16),
                pltpu.VMEM((256, 80), BF16),
                pltpu.VMEM((32, 8, 160), F32),
                pltpu.VMEM((8, 48, 128), BF16),
                pltpu.VMEM((8, 48, 128), BF16),
                pltpu.SemaphoreType.DMA((5,)),
                pltpu.SemaphoreType.DMA((8,)),
                pltpu.SemaphoreType.DMA((16,)),
                pltpu.SemaphoreType.DMA((24,)),
                pltpu.SemaphoreType.DMA,
                pltpu.SemaphoreType.DMA,
                pltpu.SemaphoreType.DMA((8,)),
                pltpu.SemaphoreType.DMA((8,)),
            ],
            compiler_params=pltpu.CompilerParams(
                collective_id=0, has_side_effects=True, vmem_limit_bytes=67_000_000
            ),
        )(pair_count, pair_target, pair_source, coeffs, translations, tmatrix)

    placed = (
        P("gz", ("gx", "gy"), None),
        P(("gx", "gz"), "gy", None),
        P("gx", "gy", None),
        P("gx"),
        P("gx"),
        P("gx"),
    )
    return jax.shard_map(
        step, mesh=mesh, in_specs=placed, out_specs=P("gz", ("gx", "gy"), None), check_vma=False
    )
```

time: 43.3 us -> 33.5 us (0.77)
  local copies, waits for them, and re-layouts: 5.74 us -> 0.61 us
  Pallas kernels: 36.6 us -> 32 us
    unnamed x11 -> x1, local copies, waits for them, and re-layouts: 5.74 us -> 0.61 us
    pallas_call x1, Pallas kernels: 36.6 us -> 32 us  [step(): pl.pallas_call(functools.partial(kernel, groups), out_shape=pltpu.VMEM(co...]
where the time goes in v3:
time: 33.5 us; the launch traced here: 33.3 us
  Pallas kernels  32 us (96%)
  between operations  0.66 us (2%)
  local copies, waits for them, and re-layouts  0.61 us (2%)
    pallas_call x1, Pallas kernels, step(): pl.pallas_call(functools.partial(kernel, groups), out_shape=pltpu.VMEM(co...  32 us

profile of v3, /device:TPU:8, one launch (start us, length us, event | category | flops | bytes accessed | tf_op | source)
XLA Modules:
  0.0 33.3 jit_solution(12836498957890354029)
XLA Ops:
  0.7 32.0 %shard_map.64 = bf16[2,16,160]{2,1,0:T(8,128)(2,1)S(1)} custom-call(s32[1]{0:T(128)S(6)} %copy.9.count, s32[512]{0:T(512)} %target_hbm.1, s32[512]{0:T(512)} %source_hbm.1, bf16[2,16,160]{2,1,0:T(8,128)(2,1)} %coeffs_hbm.1, bf16[64,80,160]{2,1,0:T(8,128)(2,1)} %trans_hbm.1, bf16[32,80,160]{2,1,0:T(8,128)(2,1)} %tmat_hbm.1), custom_call_target="tpu_custom_call" | custom-call | tf_op jit(solution)/shard_map/pallas_call | solution.py:205
  32.7 0.6 %copy.8 = bf16[2,16,160]{2,1,0:T(8,128)(2,1)} copy(bf16[2,16,160]{2,1,0:T(8,128)(2,1)S(1)} %shard_map.64) | data formatting | bytes 20480

commit v4 on v3

--- a/solution.py
+++ b/solution.py
@@ -29,7 +29,7 @@
 def kernel(
     groups, count, target_hbm, source_hbm, coeffs_hbm, trans_hbm, tmat_hbm, out,
     target, source, coeffs, trans, tmat, win, tails, pick, place, picked, contrib, near, scat, parts, sums,
-    local_sem, send_y, send_z, recv, pair_send, pair_recv, send_out, recv_out,
+    local_sem, ready, send_one, recv_y, recv_z, pair_send, pair_recv, send_out, recv_out,
 ):
     load_c = pltpu.make_async_copy(coeffs_hbm, coeffs, local_sem.at[0])
     load_c.start()
@@ -39,20 +39,29 @@
     here = gy * 4 + quarter
     half = trans_hbm.shape[0]
     pairs = 2 * half
-
-    def at(y):
-        return {"gx": gx, "gy": y // 4, "gz": (y % 4) * 2 + core}
-
-    up = {"gx": (gx + 1) % groups, "gy": gy, "gz": gz}
-    down = {"gx": (gx + groups - 1) % groups, "gy": gy, "gz": gz}
+    above, below = (gx + 1) % groups, (gx + groups - 1) % groups
+    first, last = gx % RING == 0, gx % RING == RING - 1
     sibling = {"gx": gx, "gy": gy, "gz": quarter * 2 + 1 - core}
     ring = [(here + d) % RING for d in range(RING)]
 
+    def at(group, y, c):
+        return {"gx": group, "gy": y // 4, "gz": (y % 4) * 2 + c}
+
     barrier = pltpu.get_barrier_semaphore()
+
+    def greet(peer):
+        pl.semaphore_signal(barrier, inc=1, device_id=peer, device_id_type=MESH)
+
+    greet(at(above, here, 0))
+    greet(at(below, here, 0))
+    greet(sibling)
     for d in FAR_FIRST:
-        pl.semaphore_signal(barrier, inc=1, device_id=at(ring[d]), device_id_type=MESH)
-    for peer in (up, down, sibling):
-        pl.semaphore_signal(barrier, inc=1, device_id=peer, device_id_type=MESH)
+        greet(at(gx, ring[d], 1))
+
+    @pl.when(first)
+    def _():
+        for d in FAR_FIRST:
+            greet(at(below, ring[d], 0))
 
     load_p = [
         pltpu.make_async_copy(target_hbm, target, local_sem.at[3]),
@@ -69,37 +78,72 @@
     own = coeffs[...].astype(F32).reshape(32, 160)
     win[RING + here] = packed_rows(own).astype(BF16)
 
-    pl.semaphore_wait(barrier, 10)
-
     def remote(src, dst, s, r, peer):
         return pltpu.make_async_remote_copy(
             src_ref=src, dst_ref=dst, send_sem=s, recv_sem=r, device_id=peer, device_id_type=MESH
         )
 
-    sends = []
-
-    def start(copy):
-        copy.start()
-        sends.append(copy)
+    def send_up(y, to):
+        remote(win.at[RING + y], win.at[y], send_one, recv_z.at[0], at(above, to, core)).start()
+
+    def send_down(y):
+        remote(win.at[RING + y], win.at[2 * RING + y], send_one, recv_z.at[1], at(below, here, core)).start()
 
     def forward(y):
-        block = win.at[RING + y]
-        start(remote(block, win.at[y], send_z.at[y], recv.at[y], up))
-        start(remote(block, win.at[2 * RING + y], send_z.at[RING + y], recv.at[2 * RING + y], down))
+        @pl.when(jnp.logical_not(last))
+        def _():
+            send_up(y, here)
+
+        send_down(y)
+
+    def tell_sibling():
+        pl.semaphore_signal(ready, inc=1, device_id=sibling, device_id_type=MESH)
+
+    def enter_z():
+        @pl.when(core == 0)
+        def _():
+            pl.semaphore_wait(barrier, jnp.where(last, 3 + 2 * RING, 5))
+            tell_sibling()
+
+        @pl.when(core == 1)
+        def _():
+            pl.semaphore_wait(ready, 1)
+
+    @pl.when(jnp.logical_not(first))
+    def _():
+        enter_z()
+
+        @pl.when(last)
+        def _():
+            for d in FAR_FIRST + (0,):
+                send_up(here, ring[d])
+
+        forward(here)
+
+    @pl.when(core == 1)
+    def _():
+        pl.semaphore_wait(barrier, 1 + 2 * (RING - 1))
+        tell_sibling()
+
+    @pl.when(core == 0)
+    def _():
+        pl.semaphore_wait(ready, 1)
+
+    for d in FAR_FIRST:
+        remote(
+            win.at[RING + here], win.at[RING + here], send_one, recv_y.at[RING - d], at(gx, ring[d], core)
+        ).start()
+    load_t.wait()
+    mine = trans.at[pl.ds(core * half, half)]
+    send_pair = remote(mine, mine, pair_send, pair_recv, sibling)
+    send_pair.start()
 
     def unpack(slot):
         tail = tail_rows(win[slot, 32:48, :].astype(F32)[0:8])
         tails[slot] = tail.astype(BF16)
 
-    def arrive(slot):
-        remote(win.at[slot], win.at[slot], send_y.at[0], recv.at[slot], sibling).wait_recv()
-
-    for d in FAR_FIRST:
-        start(remote(win.at[RING + here], win.at[RING + here], send_y.at[d], recv.at[RING + here], at(ring[d])))
-    forward(here)
-    load_t.wait()
-    mine = trans.at[pl.ds(core * half, half)]
-    start(remote(mine, mine, pair_send, pair_recv, sibling))
+    def received(blocks, sem):
+        remote(blocks, blocks, send_one, sem, sibling).wait_recv()
 
     for load in load_p:
         load.wait()
@@ -123,8 +167,11 @@
     lax.fori_loop(0, pairs // 8, build_pick, 0)
 
     for d in NEAR_FIRST:
-        arrive(RING + ring[d])
-        forward(ring[d])
+        received(win.at[RING + ring[d]], recv_y.at[d])
+
+        @pl.when(jnp.logical_not(first))
+        def _():
+            forward(ring[d])
 
     def build_place(q, carry):
         v = jnp.full((8, 128), -1, jnp.int32)
@@ -150,17 +197,20 @@
         chunk = jnp.dot(pick[256 * q : 256 * q + 256, 256:512], rows, preferred_element_type=F32)
         picked[256 * q : 256 * q + 256] = chunk.astype(BF16)
 
-    for d in (0,) + NEAR_FIRST:
-        arrive(ring[d])
-        arrive(2 * RING + ring[d])
-    rows = [group_rows(0), group_rows(2)]
-    for q in range(4):
-        part = pl.ds(256 * q, 256)
-        chunk = [
-            jnp.dot(pick[part, 512 * u : 512 * u + 256], rows[u], preferred_element_type=F32).astype(BF16)
-            for u in range(2)
-        ]
-        picked[part] = picked[part] + chunk[0] + chunk[1]
+    @pl.when(first)
+    def _():
+        enter_z()
+        for d in (0,) + NEAR_FIRST:
+            send_up(ring[d], here)
+            send_down(ring[d])
+
+    for g, sem in ((2, 1), (0, 0)):
+        received(win.at[8 * g : 8 * g + 8], recv_z.at[sem])
+        rows = group_rows(g)
+        for q in range(4):
+            part = pl.ds(256 * q, 256)
+            chunk = jnp.dot(pick[part, 256 * g : 256 * g + 256], rows, preferred_element_type=F32)
+            picked[part] = picked[part] + chunk.astype(BF16)
     remote(mine, trans.at[pl.ds((1 - core) * half, half)], pair_send, pair_recv, sibling).wait_recv()
 
     chosen = lax.broadcasted_iota(jnp.int32, (16, 80, 128), 2) // 8 == lax.broadcasted_iota(jnp.int32, (16, 80, 128), 0)
@@ -184,16 +234,16 @@
         rows = jnp.concatenate([scat[16 * h : 16 * h + 16, r + u, :] for u in range(2)], axis=0)
         parts[y] = packed_rows(rows).astype(BF16)
     for d in FAR_FIRST:
-        start(remote(parts.at[ring[d]], sums.at[here], send_out.at[d], recv_out.at[here], at(ring[d])))
-    total = parts[here].astype(F32)
-    for d in NEAR_FIRST:
-        y = ring[d]
-        remote(parts.at[y], sums.at[y], send_out.at[d], recv_out.at[y], sibling).wait_recv()
-        total = total + sums[y].astype(F32)
+        remote(parts.at[ring[d]], sums.at[here], send_out, recv_out, at(gx, ring[d], core)).start()
+    sums[here] = parts[here]
+    remote(parts.at[0:7], sums.at[0:7], send_out, recv_out, sibling).wait_recv()
+    total = sums[...].astype(F32).sum(axis=0)
     whole = jnp.concatenate([total[0:32], tail_rows(total[32:40])], axis=1)
     out[...] = (coeffs[...].astype(F32) - whole.reshape(2, 16, 160)).astype(BF16)
-    for copy in sends:
-        copy.wait_send()
+    remote(win.at[0:23], win.at[0:23], send_one, recv_y.at[0], sibling).wait_send()
+
+    remote(parts.at[0:7], sums.at[0:7], send_out, recv_out, sibling).wait_send()
+    send_pair.wait_send()
 
 
 def solution(mesh):
@@ -224,13 +274,14 @@
                 pltpu.VMEM((8, 48, 128), BF16),
                 pltpu.VMEM((8, 48, 128), BF16),
                 pltpu.SemaphoreType.DMA((5,)),
+                pltpu.SemaphoreType.REGULAR,
+                pltpu.SemaphoreType.DMA,
                 pltpu.SemaphoreType.DMA((8,)),
-                pltpu.SemaphoreType.DMA((16,)),
-                pltpu.SemaphoreType.DMA((24,)),
-                pltpu.SemaphoreType.DMA,
-                pltpu.SemaphoreType.DMA,
-                pltpu.SemaphoreType.DMA((8,)),
-                pltpu.SemaphoreType.DMA((8,)),
+                pltpu.SemaphoreType.DMA((2,)),
+                pltpu.SemaphoreType.DMA,
+                pltpu.SemaphoreType.DMA,
+                pltpu.SemaphoreType.DMA,
+                pltpu.SemaphoreType.DMA,
             ],
             compiler_params=pltpu.CompilerParams(
                 collective_id=0, has_side_effects=True, vmem_limit_bytes=67_000_000

time: 33.5 us -> 28.8 us (0.86)
  the two profiles are of different devices: /device:TPU:8 before, /device:TPU:1 now
where the time goes in v4:
time: 28.8 us; the launch traced here: 28.6 us
  Pallas kernels  27.3 us (95%)
  between operations  0.66 us (2%)
  local copies, waits for them, and re-layouts  0.61 us (2%)
    pallas_call x1, Pallas kernels, step(): pl.pallas_call(functools.partial(kernel, groups), out_shape=pltpu.VMEM(co...  27.3 us
    unnamed x1, local copies, waits for them, and re-layouts  0.61 us

profile of v4, /device:TPU:1, one launch (start us, length us, event | category | flops | bytes accessed | tf_op | source)
XLA Modules:
  0.0 28.6 jit_solution(467406276061542975)
XLA Ops:
  0.7 27.3 %shard_map.64 = bf16[2,16,160]{2,1,0:T(8,128)(2,1)S(1)} custom-call(s32[1]{0:T(128)S(6)} %copy.9.count, s32[512]{0:T(512)} %target_hbm.1, s32[512]{0:T(512)} %source_hbm.1, bf16[2,16,160]{2,1,0:T(8,128)(2,1)} %coeffs_hbm.1, bf16[64,80,160]{2,1,0:T(8,128)(2,1)} %trans_hbm.1, bf16[32,80,160]{2,1,0:T(8,128)(2,1)} %tmat_hbm.1), custom_call_target="tpu_custom_call" | custom-call | tf_op jit(solution)/shard_map/pallas_call | solution.py:255
  28.0 0.6 %copy.8 = bf16[2,16,160]{2,1,0:T(8,128)(2,1)} copy(bf16[2,16,160]{2,1,0:T(8,128)(2,1)S(1)} %shard_map.64) | data formatting | bytes 20480

commit v5 on v4

--- a/solution.py
+++ b/solution.py
@@ -19,7 +19,7 @@
 def packed_rows(rows):
     tails = [rows[8 * j : 8 * j + 8, 128:160] for j in range(4)]
     tail = jnp.concatenate(tails, axis=1)
-    return jnp.concatenate([rows[:, :128], tail, jnp.zeros_like(tail)], axis=0)
+    return jnp.concatenate([rows[:, :128], tail], axis=0)
 
 
 def tail_rows(tail):
@@ -28,7 +28,7 @@
 
 def kernel(
     groups, count, target_hbm, source_hbm, coeffs_hbm, trans_hbm, tmat_hbm, out,
-    target, source, coeffs, trans, tmat, win, tails, pick, place, picked, contrib, near, scat, parts, sums,
+    target, source, coeffs, trans, tmat, win, tails, ends_of, keep, pick, place, picked, near, scat, parts, sums,
     local_sem, ready, send_one, recv_y, recv_z, pair_send, pair_recv, send_out, recv_out,
 ):
     load_c = pltpu.make_async_copy(coeffs_hbm, coeffs, local_sem.at[0])
@@ -41,6 +41,8 @@
     pairs = 2 * half
     above, below = (gx + 1) % groups, (gx + groups - 1) % groups
     first, last = gx % RING == 0, gx % RING == RING - 1
+    lane = lax.broadcasted_iota(jnp.int32, (8, 128), 1)
+    sub = lax.broadcasted_iota(jnp.int32, (8, 128), 0)
     sibling = {"gx": gx, "gy": gy, "gz": quarter * 2 + 1 - core}
     ring = [(here + d) % RING for d in range(RING)]
 
@@ -139,16 +141,19 @@
     send_pair.start()
 
     def unpack(slot):
-        tail = tail_rows(win[slot, 32:48, :].astype(F32)[0:8])
-        tails[slot] = tail.astype(BF16)
+        packed = win[slot, 32:40, :].astype(F32)
+        rows = []
+        for j in range(4):
+            tail = jnp.where(lane // 32 == j, packed, 0.0)
+            tail = tail + pltpu.roll(tail, 32, 1)
+            rows.append(tail + pltpu.roll(tail, 64, 1))
+        tails[slot] = jnp.concatenate(rows, axis=0).astype(BF16)
 
     def received(blocks, sem):
         remote(blocks, blocks, send_one, sem, sibling).wait_recv()
 
     for load in load_p:
         load.wait()
-    lane = lax.broadcasted_iota(jnp.int32, (8, 128), 1)
-    sub = lax.broadcasted_iota(jnp.int32, (8, 128), 0)
     diagonal = lane - 16 * sub
 
     def build_pick(j, carry):
@@ -173,6 +178,13 @@
         def _():
             forward(ring[d])
 
+    def pack_tails(m, carry):
+        ends = [trans[8 * m + i, :, 128:160] for i in range(8)]
+        ends_of[m] = jnp.concatenate(ends, axis=1)
+        return carry
+
+    lax.fori_loop(core * 8, core * 8 + 8, pack_tails, 0)
+
     def build_place(q, carry):
         v = jnp.full((8, 128), -1, jnp.int32)
         for i in range(16):
@@ -190,7 +202,14 @@
         for y in range(RING):
             unpack(RING * g + y)
         block = win[8 * g : 8 * g + 8, 0:32, :].reshape(256, 128)
-        return jnp.concatenate([block, tails[8 * g : 8 * g + 8].reshape(256, 32)], axis=1)
+        return jnp.concatenate([block, tails[8 * g : 8 * g + 8].reshape(256, 128)], axis=1)
+
+    pair_of = lax.broadcasted_iota(jnp.int32, (128, 128), 0) // 8
+    column = lax.broadcasted_iota(jnp.int32, (128, 128), 1)
+    for u, mask in enumerate((
+        pair_of % 2 == 0, pair_of % 2 == 1, pair_of % 8 == column // 32, pair_of % 8 == column // 32 + 4,
+    )):
+        keep[u] = jnp.where(mask, 1.0, 0.0).astype(BF16)
 
     rows = group_rows(1)
     for q in range(4):
@@ -204,24 +223,56 @@
             send_up(ring[d], here)
             send_down(ring[d])
 
-    for g, sem in ((2, 1), (0, 0)):
-        received(win.at[8 * g : 8 * g + 8], recv_z.at[sem])
-        rows = group_rows(g)
-        for q in range(4):
-            part = pl.ds(256 * q, 256)
-            chunk = jnp.dot(pick[part, 256 * g : 256 * g + 256], rows, preferred_element_type=F32)
-            picked[part] = picked[part] + chunk.astype(BF16)
     remote(mine, trans.at[pl.ds((1 - core) * half, half)], pair_send, pair_recv, sibling).wait_recv()
-
-    chosen = lax.broadcasted_iota(jnp.int32, (16, 80, 128), 2) // 8 == lax.broadcasted_iota(jnp.int32, (16, 80, 128), 0)
-    for q in range(8):
-        blocks = trans[16 * q : 16 * q + 16].reshape(1280, 160)
-        every = lax.dot_general(blocks, picked[128 * q : 128 * q + 128], NT, preferred_element_type=F32)
-        every = jnp.where(chosen, every.reshape(16, 80, 128), 0.0).sum(axis=0)
-        contrib[:, 128 * q : 128 * q + 128] = every.astype(BF16)
-
-    near[...] = lax.dot_general(place[...], contrib[...], NT, preferred_element_type=F32).astype(BF16)
+    lax.fori_loop(8 - core * 8, 16 - core * 8, pack_tails, 0)
+
+    def pick_more(g, c):
+        part = pl.ds(256 * c, 256)
+        chunk = jnp.dot(pick[part, 256 * g : 256 * g + 256], rows, preferred_element_type=F32)
+        return picked[part] + chunk.astype(BF16)
+
+    received(win.at[16:24], recv_z.at[1])
+    rows = group_rows(2)
+    for c in range(4):
+        picked[256 * c : 256 * c + 256] = pick_more(2, c)
+
     load_m.wait()
+    received(win.at[0:8], recv_z.at[0])
+    rows = group_rows(0)
+    lane_of = lax.broadcasted_iota(jnp.int32, (80, 128), 1)
+    sums_at = None
+    for c in range(4):
+        both = pick_more(0, c)
+        contrib = []
+        for v in range(2):
+            q = 2 * c + v
+            mains, ends = both[128 * v : 128 * v + 128, 0:128], both[128 * v : 128 * v + 128, 128:256]
+            blocks = [
+                jnp.concatenate([trans[16 * q + 2 * j, :, 0:128], trans[16 * q + 2 * j + 1, :, 0:128]], axis=1)
+                for j in range(8)
+            ]
+            main = lax.dot_general(
+                jnp.concatenate(blocks, axis=0),
+                jnp.concatenate([mains * keep[0], mains * keep[1]], axis=1),
+                NT,
+                preferred_element_type=F32,
+            )
+            end = lax.dot_general(
+                ends_of[2 * q : 2 * q + 2].reshape(160, 256),
+                jnp.concatenate([ends * keep[2], ends * keep[3]], axis=1),
+                NT,
+                preferred_element_type=F32,
+            )
+            total = jnp.where(lane_of < 64, end[0:80], end[80:160])
+            half_sum = main[0:80]
+            for j in range(1, 8):
+                half_sum = jnp.where(lane_of // 16 == j, main[80 * j : 80 * j + 80], half_sum)
+            contrib.append((total + half_sum).astype(BF16))
+        part = lax.dot_general(
+            place[:, 256 * c : 256 * c + 256], jnp.concatenate(contrib, axis=1), NT, preferred_element_type=F32
+        )
+        sums_at = part if sums_at is None else sums_at + part
+    near[...] = sums_at.astype(BF16)
 
     for j in range(16):
         rows = near[16 * j : 16 * j + 16, :]
@@ -263,16 +314,17 @@
                 pltpu.VMEM(coeffs.shape, BF16),
                 pltpu.VMEM((2 * half, 80, 160), BF16),
                 pltpu.VMEM((32, 80, 160), BF16),
-                pltpu.VMEM((24, 48, 128), BF16),
-                pltpu.VMEM((24, 32, 32), BF16),
+                pltpu.VMEM((24, 40, 128), BF16),
+                pltpu.VMEM((24, 32, 128), BF16),
+                pltpu.VMEM((16, 80, 256), BF16),
+                pltpu.VMEM((4, 128, 128), BF16),
                 pltpu.VMEM((1024, 768), BF16),
                 pltpu.VMEM((256, 1024), BF16),
-                pltpu.VMEM((1024, 160), BF16),
-                pltpu.VMEM((80, 1024), BF16),
+                pltpu.VMEM((1024, 256), BF16),
                 pltpu.VMEM((256, 80), BF16),
                 pltpu.VMEM((32, 8, 160), F32),
-                pltpu.VMEM((8, 48, 128), BF16),
-                pltpu.VMEM((8, 48, 128), BF16),
+                pltpu.VMEM((8, 40, 128), BF16),
+                pltpu.VMEM((8, 40, 128), BF16),
                 pltpu.SemaphoreType.DMA((5,)),
                 pltpu.SemaphoreType.REGULAR,
                 pltpu.SemaphoreType.DMA,

time: 28.8 us -> 28.4 us (0.986)
  Pallas kernels: 27.3 us -> 26.9 us
    pallas_call x1, Pallas kernels: 27.3 us -> 26.9 us  [step(): pl.pallas_call(functools.partial(kernel, groups), out_shape=pltpu.VMEM(co...]
where the time goes in v5:
time: 28.4 us; the launch traced here: 28.2 us
  Pallas kernels  26.9 us (95%)
  between operations  0.66 us (2%)
  local copies, waits for them, and re-layouts  0.61 us (2%)
    pallas_call x1, Pallas kernels, step(): pl.pallas_call(functools.partial(kernel, groups), out_shape=pltpu.VMEM(co...  26.9 us
    unnamed x1, local copies, waits for them, and re-layouts  0.61 us

profile of v5, /device:TPU:1, one launch (start us, length us, event | category | flops | bytes accessed | tf_op | source)
XLA Modules:
  0.0 28.2 jit_solution(17445917168656265464)
XLA Ops:
  0.7 26.9 %shard_map.64 = bf16[2,16,160]{2,1,0:T(8,128)(2,1)S(1)} custom-call(s32[1]{0:T(128)S(6)} %copy.9.count, s32[512]{0:T(512)} %target_hbm.1, s32[512]{0:T(512)} %source_hbm.1, bf16[2,16,160]{2,1,0:T(8,128)(2,1)} %coeffs_hbm.1, bf16[64,80,160]{2,1,0:T(8,128)(2,1)} %trans_hbm.1, bf16[32,80,160]{2,1,0:T(8,128)(2,1)} %tmat_hbm.1), custom_call_target="tpu_custom_call" | custom-call | tf_op jit(solution)/shard_map/pallas_call | solution.py:306
  27.6 0.6 %copy.8 = bf16[2,16,160]{2,1,0:T(8,128)(2,1)} copy(bf16[2,16,160]{2,1,0:T(8,128)(2,1)S(1)} %shard_map.64) | data formatting | bytes 20480

commit v6 on v5

--- a/solution.py
+++ b/solution.py
@@ -76,6 +76,19 @@
     load_t.start()
     load_m.start()
 
+    def tell_sibling():
+        pl.semaphore_signal(ready, inc=1, device_id=sibling, device_id_type=MESH)
+
+    def hear_z():
+        @pl.when(core == 0)
+        def _():
+            pl.semaphore_wait(barrier, jnp.where(last, 3 + 2 * RING, 5))
+            tell_sibling()
+
+    @pl.when(jnp.logical_not(first))
+    def _():
+        hear_z()
+
     load_c.wait()
     own = coeffs[...].astype(F32).reshape(32, 160)
     win[RING + here] = packed_rows(own).astype(BF16)
@@ -98,22 +111,11 @@
 
         send_down(y)
 
-    def tell_sibling():
-        pl.semaphore_signal(ready, inc=1, device_id=sibling, device_id_type=MESH)
-
-    def enter_z():
-        @pl.when(core == 0)
-        def _():
-            pl.semaphore_wait(barrier, jnp.where(last, 3 + 2 * RING, 5))
-            tell_sibling()
-
+    @pl.when(jnp.logical_not(first))
+    def _():
         @pl.when(core == 1)
         def _():
             pl.semaphore_wait(ready, 1)
-
-    @pl.when(jnp.logical_not(first))
-    def _():
-        enter_z()
 
         @pl.when(last)
         def _():
@@ -218,7 +220,12 @@
 
     @pl.when(first)
     def _():
-        enter_z()
+        hear_z()
+
+        @pl.when(core == 1)
+        def _():
+            pl.semaphore_wait(ready, 1)
+
         for d in (0,) + NEAR_FIRST:
             send_up(ring[d], here)
             send_down(ring[d])

time: 28.4 us -> 27.6 us (0.972)
  the two profiles are of different devices: /device:TPU:1 before, /device:TPU:8 now
where the time goes in v6:
time: 27.6 us; the launch traced here: 27.5 us
  Pallas kernels  26.2 us (95%)
  between operations  0.66 us (2%)
  local copies, waits for them, and re-layouts  0.61 us (2%)
    pallas_call x1, Pallas kernels, step(): pl.pallas_call(functools.partial(kernel, groups), out_shape=pltpu.VMEM(co...  26.2 us
    unnamed x1, local copies, waits for them, and re-layouts  0.61 us

profile of v6, /device:TPU:8, one launch (start us, length us, event | category | flops | bytes accessed | tf_op | source)
XLA Modules:
  0.0 27.5 jit_solution(6765071798090623781)
XLA Ops:
  0.7 26.2 %shard_map.64 = bf16[2,16,160]{2,1,0:T(8,128)(2,1)S(1)} custom-call(s32[1]{0:T(128)S(6)} %copy.9.count, s32[512]{0:T(512)} %target_hbm.1, s32[512]{0:T(512)} %source_hbm.1, bf16[2,16,160]{2,1,0:T(8,128)(2,1)} %coeffs_hbm.1, bf16[64,80,160]{2,1,0:T(8,128)(2,1)} %trans_hbm.1, bf16[32,80,160]{2,1,0:T(8,128)(2,1)} %tmat_hbm.1), custom_call_target="tpu_custom_call" | custom-call | tf_op jit(solution)/shard_map/pallas_call | solution.py:313
  26.8 0.6 %copy.8 = bf16[2,16,160]{2,1,0:T(8,128)(2,1)} copy(bf16[2,16,160]{2,1,0:T(8,128)(2,1)S(1)} %shard_map.64) | data formatting | bytes 20480

commit v7 on v6

--- a/solution.py
+++ b/solution.py
@@ -28,7 +28,7 @@
 
 def kernel(
     groups, count, target_hbm, source_hbm, coeffs_hbm, trans_hbm, tmat_hbm, out,
-    target, source, coeffs, trans, tmat, win, tails, ends_of, keep, pick, place, picked, near, scat, parts, sums,
+    target, source, coeffs, trans, tmat, win, tails, ends_of, keep, pick, place, picked, wide, scat, parts, sums,
     local_sem, ready, send_one, recv_y, recv_z, pair_send, pair_recv, send_out, recv_out,
 ):
     load_c = pltpu.make_async_copy(coeffs_hbm, coeffs, local_sem.at[0])
@@ -144,11 +144,13 @@
 
     def unpack(slot):
         packed = win[slot, 32:40, :].astype(F32)
+        turned = [packed] + [pltpu.roll(packed, 32 * j, 1) for j in range(1, 4)]
         rows = []
         for j in range(4):
-            tail = jnp.where(lane // 32 == j, packed, 0.0)
-            tail = tail + pltpu.roll(tail, 32, 1)
-            rows.append(tail + pltpu.roll(tail, 64, 1))
+            tail = turned[(3 - j) % 4]
+            for v in range(3):
+                tail = jnp.where(lane // 32 == v, turned[(v - j) % 4], tail)
+            rows.append(tail)
         tails[slot] = jnp.concatenate(rows, axis=0).astype(BF16)
 
     def received(blocks, sem):
@@ -173,19 +175,16 @@
 
     lax.fori_loop(0, pairs // 8, build_pick, 0)
 
-    for d in NEAR_FIRST:
-        received(win.at[RING + ring[d]], recv_y.at[d])
-
-        @pl.when(jnp.logical_not(first))
-        def _():
-            forward(ring[d])
-
     def pack_tails(m, carry):
         ends = [trans[8 * m + i, :, 128:160] for i in range(8)]
         ends_of[m] = jnp.concatenate(ends, axis=1)
         return carry
 
-    lax.fori_loop(core * 8, core * 8 + 8, pack_tails, 0)
+    def repeat_ends(m, carry):
+        for u in range(4):
+            block = tmat[4 * m + u]
+            wide[4 * m + u] = jnp.concatenate([block[:, 0:128]] + [block[:, 128:160]] * 4, axis=1)
+        return carry
 
     def build_place(q, carry):
         v = jnp.full((8, 128), -1, jnp.int32)
@@ -198,7 +197,26 @@
             place[16 * s : 16 * s + 16, pl.ds(pl.multiple_of(128 * q, 128), 128)] = jnp.concatenate(hot, axis=0).astype(BF16)
         return carry
 
-    lax.fori_loop(0, pairs // 16, build_place, 0)
+    def prepare():
+        lax.fori_loop(core * 8, core * 8 + 8, pack_tails, 0)
+        load_m.wait()
+        lax.fori_loop(0, 8, repeat_ends, 0)
+        lax.fori_loop(0, pairs // 16, build_place, 0)
+
+    @pl.when(first)
+    def _():
+        prepare()
+
+    for d in NEAR_FIRST:
+        received(win.at[RING + ring[d]], recv_y.at[d])
+
+        @pl.when(jnp.logical_not(first))
+        def _():
+            forward(ring[d])
+
+    @pl.when(jnp.logical_not(first))
+    def _():
+        prepare()
 
     def group_rows(g):
         for y in range(RING):
@@ -243,7 +261,6 @@
     for c in range(4):
         picked[256 * c : 256 * c + 256] = pick_more(2, c)
 
-    load_m.wait()
     received(win.at[0:8], recv_z.at[0])
     rows = group_rows(0)
     lane_of = lax.broadcasted_iota(jnp.int32, (80, 128), 1)
@@ -279,18 +296,21 @@
             place[:, 256 * c : 256 * c + 256], jnp.concatenate(contrib, axis=1), NT, preferred_element_type=F32
         )
         sums_at = part if sums_at is None else sums_at + part
-    near[...] = sums_at.astype(BF16)
+    near = sums_at.astype(BF16)
 
     for j in range(16):
-        rows = near[16 * j : 16 * j + 16, :]
         for u in range(2):
-            both = jnp.dot(rows, tmat[2 * j + u], preferred_element_type=F32)
+            both = jnp.dot(near[16 * j : 16 * j + 16], wide[2 * j + u], preferred_element_type=F32)
             scat[2 * j + u] = both[8 * u : 8 * u + 8]
 
     for y in range(RING):
-        h, r = y // 4, 2 * (y % 4)
-        rows = jnp.concatenate([scat[16 * h : 16 * h + 16, r + u, :] for u in range(2)], axis=0)
-        parts[y] = packed_rows(rows).astype(BF16)
+        h, r = 16 * (y // 4), 2 * (y % 4)
+        rows = [scat[h : h + 16, r + u, 0:128] for u in range(2)]
+        ends = [scat[h + 8 * (j % 2) : h + 8 * (j % 2) + 8, r + j // 2, 128:256] for j in range(4)]
+        tail = ends[3]
+        for v in range(3):
+            tail = jnp.where(lane // 32 == v, ends[v], tail)
+        parts[y] = jnp.concatenate(rows + [tail], axis=0).astype(BF16)
     for d in FAR_FIRST:
         remote(parts.at[ring[d]], sums.at[here], send_out, recv_out, at(gx, ring[d], core)).start()
     sums[here] = parts[here]
@@ -328,8 +348,8 @@
                 pltpu.VMEM((1024, 768), BF16),
                 pltpu.VMEM((256, 1024), BF16),
                 pltpu.VMEM((1024, 256), BF16),
-                pltpu.VMEM((256, 80), BF16),
-                pltpu.VMEM((32, 8, 160), F32),
+                pltpu.VMEM((32, 80, 256), BF16),
+                pltpu.VMEM((32, 8, 256), F32),
                 pltpu.VMEM((8, 40, 128), BF16),
                 pltpu.VMEM((8, 40, 128), BF16),
                 pltpu.SemaphoreType.DMA((5,)),

time: 27.6 us -> 27.5 us (level)
  no operation moved by 1% of the time
where the time goes in v7:
time: 27.5 us; the launch traced here: 27.3 us
  Pallas kernels  26 us (95%)
  between operations  0.66 us (2%)
  local copies, waits for them, and re-layouts  0.61 us (2%)
    pallas_call x1, Pallas kernels, step(): pl.pallas_call(functools.partial(kernel, groups), out_shape=pltpu.VMEM(co...  26 us
    unnamed x1, local copies, waits for them, and re-layouts  0.61 us

profile of v7, /device:TPU:8, one launch (start us, length us, event | category | flops | bytes accessed | tf_op | source)
XLA Modules:
  0.0 27.3 jit_solution(5583489200381530484)
XLA Ops:
  0.7 26.0 %shard_map.64 = bf16[2,16,160]{2,1,0:T(8,128)(2,1)S(1)} custom-call(s32[1]{0:T(128)S(6)} %copy.9.count, s32[512]{0:T(512)} %target_hbm.1, s32[512]{0:T(512)} %source_hbm.1, bf16[2,16,160]{2,1,0:T(8,128)(2,1)} %coeffs_hbm.1, bf16[64,80,160]{2,1,0:T(8,128)(2,1)} %trans_hbm.1, bf16[32,80,160]{2,1,0:T(8,128)(2,1)} %tmat_hbm.1), custom_call_target="tpu_custom_call" | custom-call | tf_op jit(solution)/shard_map/pallas_call | solution.py:333
  26.7 0.6 %copy.8 = bf16[2,16,160]{2,1,0:T(8,128)(2,1)} copy(bf16[2,16,160]{2,1,0:T(8,128)(2,1)S(1)} %shard_map.64) | data formatting | bytes 20480

commit v8 on v7

--- a/solution.py
+++ b/solution.py
@@ -28,7 +28,7 @@
 
 def kernel(
     groups, count, target_hbm, source_hbm, coeffs_hbm, trans_hbm, tmat_hbm, out,
-    target, source, coeffs, trans, tmat, win, tails, ends_of, keep, pick, place, picked, wide, scat, parts, sums,
+    target, source, coeffs, trans, tmat, win, window, ends_of, place, wide, scat, parts, sums,
     local_sem, ready, send_one, recv_y, recv_z, pair_send, pair_recv, send_out, recv_out,
 ):
     load_c = pltpu.make_async_copy(coeffs_hbm, coeffs, local_sem.at[0])
@@ -142,38 +142,22 @@
     send_pair = remote(mine, mine, pair_send, pair_recv, sibling)
     send_pair.start()
 
-    def unpack(slot):
-        packed = win[slot, 32:40, :].astype(F32)
-        turned = [packed] + [pltpu.roll(packed, 32 * j, 1) for j in range(1, 4)]
-        rows = []
-        for j in range(4):
-            tail = turned[(3 - j) % 4]
-            for v in range(3):
-                tail = jnp.where(lane // 32 == v, turned[(v - j) % 4], tail)
-            rows.append(tail)
-        tails[slot] = jnp.concatenate(rows, axis=0).astype(BF16)
+    def unpack(group):
+        for y in range(RING):
+            block = win[RING * group + y].astype(F32)
+            base, r = 32 * group + 16 * (y // 4), 2 * (y % 4)
+            packed = block[32:40]
+            turned = [packed] + [pltpu.roll(packed, 32 * j, 1) for j in range(1, 4)]
+            for j in range(4):
+                tail = turned[(3 - j) % 4]
+                for v in range(3):
+                    tail = jnp.where(lane // 32 == v, turned[(v - j) % 4], tail)
+                rows = pl.ds(base + 8 * (j % 2), 8)
+                window[rows, r + j // 2, 0:128] = block[8 * j : 8 * j + 8]
+                window[rows, r + j // 2, 128:256] = tail
 
     def received(blocks, sem):
         remote(blocks, blocks, send_one, sem, sibling).wait_recv()
-
-    for load in load_p:
-        load.wait()
-    diagonal = lane - 16 * sub
-
-    def build_pick(j, carry):
-        for v in range(4):
-            codes = []
-            for u in range(2):
-                s = source[quarter * pairs + 8 * j + 2 * v + u]
-                relative = (s // 32 - gx + 1 + groups) % groups
-                codes.append((relative * 2 + (s % 32) // 16) * 1024 + s % 16)
-            rows = pl.ds(pl.multiple_of(64 * j + 16 * v, 16), 16)
-            for t in range(6):
-                hot = [jnp.where(diagonal == c - 1024 * t, 1.0, 0.0) for c in codes]
-                pick[rows, 128 * t : 128 * t + 128] = jnp.concatenate(hot, axis=0).astype(BF16)
-        return carry
-
-    lax.fori_loop(0, pairs // 8, build_pick, 0)
 
     def pack_tails(m, carry):
         ends = [trans[8 * m + i, :, 128:160] for i in range(8)]
@@ -198,6 +182,8 @@
         return carry
 
     def prepare():
+        for load in load_p:
+            load.wait()
         lax.fori_loop(core * 8, core * 8 + 8, pack_tails, 0)
         load_m.wait()
         lax.fori_loop(0, 8, repeat_ends, 0)
@@ -224,17 +210,7 @@
         block = win[8 * g : 8 * g + 8, 0:32, :].reshape(256, 128)
         return jnp.concatenate([block, tails[8 * g : 8 * g + 8].reshape(256, 128)], axis=1)
 
-    pair_of = lax.broadcasted_iota(jnp.int32, (128, 128), 0) // 8
-    column = lax.broadcasted_iota(jnp.int32, (128, 128), 1)
-    for u, mask in enumerate((
-        pair_of % 2 == 0, pair_of % 2 == 1, pair_of % 8 == column // 32, pair_of % 8 == column // 32 + 4,
-    )):
-        keep[u] = jnp.where(mask, 1.0, 0.0).astype(BF16)
-
-    rows = group_rows(1)
-    for q in range(4):
-        chunk = jnp.dot(pick[256 * q : 256 * q + 256, 256:512], rows, preferred_element_type=F32)
-        picked[256 * q : 256 * q + 256] = chunk.astype(BF16)
+    unpack(1)
 
     @pl.when(first)
     def _():
@@ -251,39 +227,50 @@
     remote(mine, trans.at[pl.ds((1 - core) * half, half)], pair_send, pair_recv, sibling).wait_recv()
     lax.fori_loop(8 - core * 8, 16 - core * 8, pack_tails, 0)
 
-    def pick_more(g, c):
-        part = pl.ds(256 * c, 256)
-        chunk = jnp.dot(pick[part, 256 * g : 256 * g + 256], rows, preferred_element_type=F32)
-        return picked[part] + chunk.astype(BF16)
-
     received(win.at[16:24], recv_z.at[1])
-    rows = group_rows(2)
-    for c in range(4):
-        picked[256 * c : 256 * c + 256] = pick_more(2, c)
+    unpack(2)
+    spheres = 32 * groups
+    shift = spheres + 32 - 32 * gx
+    nothing = jnp.zeros((8, 128), F32)
+
+    def picked_rows(q):
+        mains, ends = [], []
+        for i in range(0, 16, 2):
+            pair = []
+            for u in range(2):
+                s = source[quarter * pairs + 16 * q + i + u]
+                pair.append(window[jnp.minimum(lax.rem(s + shift, spheres), 95)])
+            mains += [
+                jnp.concatenate([pair[0][:, 0:128], nothing], axis=1),
+                jnp.concatenate([nothing, pair[1][:, 0:128]], axis=1),
+            ]
+            for u in range(2):
+                end = jnp.where(lane // 32 == (i + u) % 4, pair[u][:, 128:256], 0.0)
+                ends.append(jnp.concatenate([end, nothing] if i % 8 < 4 else [nothing, end], axis=1))
+        return jnp.concatenate(mains, axis=0).astype(BF16), jnp.concatenate(ends, axis=0).astype(BF16)
 
     received(win.at[0:8], recv_z.at[0])
-    rows = group_rows(0)
+    unpack(0)
     lane_of = lax.broadcasted_iota(jnp.int32, (80, 128), 1)
     sums_at = None
     for c in range(4):
-        both = pick_more(0, c)
         contrib = []
         for v in range(2):
             q = 2 * c + v
-            mains, ends = both[128 * v : 128 * v + 128, 0:128], both[128 * v : 128 * v + 128, 128:256]
+            mains, ends = picked_rows(q)
             blocks = [
                 jnp.concatenate([trans[16 * q + 2 * j, :, 0:128], trans[16 * q + 2 * j + 1, :, 0:128]], axis=1)
                 for j in range(8)
             ]
             main = lax.dot_general(
                 jnp.concatenate(blocks, axis=0),
-                jnp.concatenate([mains * keep[0], mains * keep[1]], axis=1),
+                mains,
                 NT,
                 preferred_element_type=F32,
             )
             end = lax.dot_general(
                 ends_of[2 * q : 2 * q + 2].reshape(160, 256),
-                jnp.concatenate([ends * keep[2], ends * keep[3]], axis=1),
+                ends,
                 NT,
                 preferred_element_type=F32,
             )
@@ -342,12 +329,9 @@
                 pltpu.VMEM((2 * half, 80, 160), BF16),
                 pltpu.VMEM((32, 80, 160), BF16),
                 pltpu.VMEM((24, 40, 128), BF16),
-                pltpu.VMEM((24, 32, 128), BF16),
+                pltpu.VMEM((96, 8, 256), F32),
                 pltpu.VMEM((16, 80, 256), BF16),
-                pltpu.VMEM((4, 128, 128), BF16),
-                pltpu.VMEM((1024, 768), BF16),
                 pltpu.VMEM((256, 1024), BF16),
-                pltpu.VMEM((1024, 256), BF16),
                 pltpu.VMEM((32, 80, 256), BF16),
                 pltpu.VMEM((32, 8, 256), F32),
                 pltpu.VMEM((8, 40, 128), BF16),

time: 27.5 us -> 27.1 us (0.985)
  Pallas kernels: 26 us -> 25.6 us
    pallas_call x1, Pallas kernels: 26 us -> 25.6 us  [step(): pl.pallas_call(functools.partial(kernel, groups), out_shape=pltpu.VMEM(co...]
where the time goes in v8:
time: 27.1 us; the launch traced here: 26.9 us
  Pallas kernels  25.6 us (94%)
  between operations  0.66 us (2%)
  local copies, waits for them, and re-layouts  0.61 us (2%)
    pallas_call x1, Pallas kernels, step(): pl.pallas_call(functools.partial(kernel, groups), out_shape=pltpu.VMEM(co...  25.6 us
    unnamed x1, local copies, waits for them, and re-layouts  0.61 us

profile of v8, /device:TPU:8, one launch (start us, length us, event | category | flops | bytes accessed | tf_op | source)
XLA Modules:
  0.0 26.9 jit_solution(3500137266460739268)
XLA Ops:
  0.7 25.6 %shard_map.64 = bf16[2,16,160]{2,1,0:T(8,128)(2,1)S(1)} custom-call(s32[1]{0:T(128)S(6)} %copy.9.count, s32[512]{0:T(512)} %target_hbm.1, s32[512]{0:T(512)} %source_hbm.1, bf16[2,16,160]{2,1,0:T(8,128)(2,1)} %coeffs_hbm.1, bf16[64,80,160]{2,1,0:T(8,128)(2,1)} %trans_hbm.1, bf16[32,80,160]{2,1,0:T(8,128)(2,1)} %tmat_hbm.1), custom_call_target="tpu_custom_call" | custom-call | tf_op jit(solution)/shard_map/pallas_call | solution.py:320
  26.3 0.6 %copy.8 = bf16[2,16,160]{2,1,0:T(8,128)(2,1)} copy(bf16[2,16,160]{2,1,0:T(8,128)(2,1)S(1)} %shard_map.64) | data formatting | bytes 20480

commit v9 on v8

--- a/solution.py
+++ b/solution.py
@@ -54,7 +54,14 @@
     def greet(peer):
         pl.semaphore_signal(barrier, inc=1, device_id=peer, device_id_type=MESH)
 
-    greet(at(above, here, 0))
+    @pl.when(gx % RING == RING - 2)
+    def _():
+        greet(at(above, here, 1))
+
+    @pl.when(gx % RING != RING - 2)
+    def _():
+        greet(at(above, here, 0))
+
     greet(at(below, here, 0))
     greet(sibling)
     for d in FAR_FIRST:
@@ -82,7 +89,7 @@
     def hear_z():
         @pl.when(core == 0)
         def _():
-            pl.semaphore_wait(barrier, jnp.where(last, 3 + 2 * RING, 5))
+            pl.semaphore_wait(barrier, jnp.where(last, 1 + 2 * RING, 5))
             tell_sibling()
 
     @pl.when(jnp.logical_not(first))
@@ -99,7 +106,7 @@
         )
 
     def send_up(y, to):
-        remote(win.at[RING + y], win.at[y], send_one, recv_z.at[0], at(above, to, core)).start()
+        remote(win.at[RING + y], win.at[y], send_one, recv_z.at[2 * (y // 4)], at(above, to, core)).start()
 
     def send_down(y):
         remote(win.at[RING + y], win.at[2 * RING + y], send_one, recv_z.at[1], at(below, here, core)).start()
@@ -122,11 +129,13 @@
             for d in FAR_FIRST + (0,):
                 send_up(here, ring[d])
 
-        forward(here)
+        @pl.when(jnp.logical_not(last))
+        def _():
+            forward(here)
 
     @pl.when(core == 1)
     def _():
-        pl.semaphore_wait(barrier, 1 + 2 * (RING - 1))
+        pl.semaphore_wait(barrier, jnp.where(last, 1 + 2 * RING, 2 * RING - 1))
         tell_sibling()
 
     @pl.when(core == 0)
@@ -137,13 +146,18 @@
         remote(
             win.at[RING + here], win.at[RING + here], send_one, recv_y.at[RING - d], at(gx, ring[d], core)
         ).start()
+
+    @pl.when(last)
+    def _():
+        send_down(here)
+
     load_t.wait()
     mine = trans.at[pl.ds(core * half, half)]
     send_pair = remote(mine, mine, pair_send, pair_recv, sibling)
     send_pair.start()
 
-    def unpack(group):
-        for y in range(RING):
+    def unpack(group, blocks=range(RING)):
+        for y in blocks:
             block = win[RING * group + y].astype(F32)
             base, r = 32 * group + 16 * (y // 4), 2 * (y % 4)
             packed = block[32:40]
@@ -249,8 +263,10 @@
                 ends.append(jnp.concatenate([end, nothing] if i % 8 < 4 else [nothing, end], axis=1))
         return jnp.concatenate(mains, axis=0).astype(BF16), jnp.concatenate(ends, axis=0).astype(BF16)
 
-    received(win.at[0:8], recv_z.at[0])
-    unpack(0)
+    received(win.at[0:4], recv_z.at[0])
+    unpack(0, range(4))
+    received(win.at[4:8], recv_z.at[2])
+    unpack(0, range(4, 8))
     lane_of = lax.broadcasted_iota(jnp.int32, (80, 128), 1)
     sums_at = None
     for c in range(4):
@@ -340,7 +356,7 @@
                 pltpu.SemaphoreType.REGULAR,
                 pltpu.SemaphoreType.DMA,
                 pltpu.SemaphoreType.DMA((8,)),
-                pltpu.SemaphoreType.DMA((2,)),
+                pltpu.SemaphoreType.DMA((3,)),
                 pltpu.SemaphoreType.DMA,
                 pltpu.SemaphoreType.DMA,
                 pltpu.SemaphoreType.DMA,

time: 27.1 us -> 26.7 us (0.985)
  Pallas kernels: 25.6 us -> 25.2 us
    pallas_call x1, Pallas kernels: 25.6 us -> 25.2 us  [step(): pl.pallas_call(functools.partial(kernel, groups), out_shape=pltpu.VMEM(co...]
where the time goes in v9:
time: 26.7 us; the launch traced here: 26.5 us
  Pallas kernels  25.2 us (94%)
  between operations  0.66 us (2%)
  local copies, waits for them, and re-layouts  0.61 us (2%)
    pallas_call x1, Pallas kernels, step(): pl.pallas_call(functools.partial(kernel, groups), out_shape=pltpu.VMEM(co...  25.2 us
    unnamed x1, local copies, waits for them, and re-layouts  0.61 us

profile of v9, /device:TPU:8, one launch (start us, length us, event | category | flops | bytes accessed | tf_op | source)
XLA Modules:
  0.0 26.5 jit_solution(12083180034317775385)
XLA Ops:
  0.7 25.2 %shard_map.64 = bf16[2,16,160]{2,1,0:T(8,128)(2,1)S(1)} custom-call(s32[1]{0:T(128)S(6)} %copy.9.count, s32[512]{0:T(512)} %target_hbm.1, s32[512]{0:T(512)} %source_hbm.1, bf16[2,16,160]{2,1,0:T(8,128)(2,1)} %coeffs_hbm.1, bf16[64,80,160]{2,1,0:T(8,128)(2,1)} %trans_hbm.1, bf16[32,80,160]{2,1,0:T(8,128)(2,1)} %tmat_hbm.1), custom_call_target="tpu_custom_call" | custom-call | tf_op jit(solution)/shard_map/pallas_call | solution.py:336
  25.9 0.6 %copy.8 = bf16[2,16,160]{2,1,0:T(8,128)(2,1)} copy(bf16[2,16,160]{2,1,0:T(8,128)(2,1)S(1)} %shard_map.64) | data formatting | bytes 20480

commit v10 on v9

--- a/solution.py
+++ b/solution.py
@@ -29,8 +29,9 @@
 def kernel(
     groups, count, target_hbm, source_hbm, coeffs_hbm, trans_hbm, tmat_hbm, out,
     target, source, coeffs, trans, tmat, win, window, ends_of, place, wide, scat, parts, sums,
-    local_sem, ready, send_one, recv_y, recv_z, pair_send, pair_recv, send_out, recv_out,
+    local_sem, ready, recv_y, recv_z, pair_recv, recv_out,
 ):
+    send_one, pair_send, send_out = local_sem.at[0], local_sem.at[1], local_sem.at[2]
     load_c = pltpu.make_async_copy(coeffs_hbm, coeffs, local_sem.at[0])
     load_c.start()
 
@@ -144,7 +145,7 @@
 
     for d in FAR_FIRST:
         remote(
-            win.at[RING + here], win.at[RING + here], send_one, recv_y.at[RING - d], at(gx, ring[d], core)
+            win.at[RING + here], win.at[RING + here], send_one, recv_y.at[RING - 1 - d], at(gx, ring[d], core)
         ).start()
 
     @pl.when(last)
@@ -208,7 +209,7 @@
         prepare()
 
     for d in NEAR_FIRST:
-        received(win.at[RING + ring[d]], recv_y.at[d])
+        received(win.at[RING + ring[d]], recv_y.at[d - 1])
 
         @pl.when(jnp.logical_not(first))
         def _():
@@ -354,11 +355,8 @@
                 pltpu.VMEM((8, 40, 128), BF16),
                 pltpu.SemaphoreType.DMA((5,)),
                 pltpu.SemaphoreType.REGULAR,
-                pltpu.SemaphoreType.DMA,
-                pltpu.SemaphoreType.DMA((8,)),
+                pltpu.SemaphoreType.DMA((RING - 1,)),
                 pltpu.SemaphoreType.DMA((3,)),
-                pltpu.SemaphoreType.DMA,
-                pltpu.SemaphoreType.DMA,
                 pltpu.SemaphoreType.DMA,
                 pltpu.SemaphoreType.DMA,
             ],

time: 26.7 us -> 26.6 us (level)
  no operation moved by 1% of the time
where the time goes in v10:
time: 26.6 us; the launch traced here: 26.4 us
  Pallas kernels  25.2 us (95%)
  between operations  0.66 us (2%)
  local copies, waits for them, and re-layouts  0.61 us (2%)
    pallas_call x1, Pallas kernels, step(): pl.pallas_call(functools.partial(kernel, groups), out_shape=pltpu.VMEM(co...  25.2 us
    unnamed x1, local copies, waits for them, and re-layouts  0.61 us

profile of v10, /device:TPU:8, one launch (start us, length us, event | category | flops | bytes accessed | tf_op | source)
XLA Modules:
  0.0 26.4 jit_solution(5214331260738779594)
XLA Ops:
  0.7 25.2 %shard_map.64 = bf16[2,16,160]{2,1,0:T(8,128)(2,1)S(1)} custom-call(s32[1]{0:T(128)S(6)} %copy.9.count, s32[512]{0:T(512)} %target_hbm.1, s32[512]{0:T(512)} %source_hbm.1, bf16[2,16,160]{2,1,0:T(8,128)(2,1)} %coeffs_hbm.1, bf16[64,80,160]{2,1,0:T(8,128)(2,1)} %trans_hbm.1, bf16[32,80,160]{2,1,0:T(8,128)(2,1)} %tmat_hbm.1), custom_call_target="tpu_custom_call" | custom-call | tf_op jit(solution)/shard_map/pallas_call | solution.py:337
  25.8 0.6 %copy.8 = bf16[2,16,160]{2,1,0:T(8,128)(2,1)} copy(bf16[2,16,160]{2,1,0:T(8,128)(2,1)S(1)} %shard_map.64) | data formatting | bytes 20480

commit v11 on v10

--- a/solution.py
+++ b/solution.py
@@ -107,10 +107,10 @@
         )
 
     def send_up(y, to):
-        remote(win.at[RING + y], win.at[y], send_one, recv_z.at[2 * (y // 4)], at(above, to, core)).start()
+        remote(win.at[RING + y], win.at[y], send_one, recv_z.at[y // 2], at(above, to, core)).start()
 
     def send_down(y):
-        remote(win.at[RING + y], win.at[2 * RING + y], send_one, recv_z.at[1], at(below, here, core)).start()
+        remote(win.at[RING + y], win.at[2 * RING + y], send_one, recv_z.at[4], at(below, here, core)).start()
 
     def forward(y):
         @pl.when(jnp.logical_not(last))
@@ -242,7 +242,7 @@
     remote(mine, trans.at[pl.ds((1 - core) * half, half)], pair_send, pair_recv, sibling).wait_recv()
     lax.fori_loop(8 - core * 8, 16 - core * 8, pack_tails, 0)
 
-    received(win.at[16:24], recv_z.at[1])
+    received(win.at[16:24], recv_z.at[4])
     unpack(2)
     spheres = 32 * groups
     shift = spheres + 32 - 32 * gx
@@ -264,10 +264,9 @@
                 ends.append(jnp.concatenate([end, nothing] if i % 8 < 4 else [nothing, end], axis=1))
         return jnp.concatenate(mains, axis=0).astype(BF16), jnp.concatenate(ends, axis=0).astype(BF16)
 
-    received(win.at[0:4], recv_z.at[0])
-    unpack(0, range(4))
-    received(win.at[4:8], recv_z.at[2])
-    unpack(0, range(4, 8))
+    for v in (0, 1, 3, 2):
+        received(win.at[2 * v : 2 * v + 2], recv_z.at[v])
+        unpack(0, range(2 * v, 2 * v + 2))
     lane_of = lax.broadcasted_iota(jnp.int32, (80, 128), 1)
     sums_at = None
     for c in range(4):
@@ -356,7 +355,7 @@
                 pltpu.SemaphoreType.DMA((5,)),
                 pltpu.SemaphoreType.REGULAR,
                 pltpu.SemaphoreType.DMA((RING - 1,)),
-                pltpu.SemaphoreType.DMA((3,)),
+                pltpu.SemaphoreType.DMA((5,)),
                 pltpu.SemaphoreType.DMA,
                 pltpu.SemaphoreType.DMA,
             ],

time: 26.6 us -> 26.6 us (level)
  no operation moved by 1% of the time
where the time goes in v11:
time: 26.6 us; the launch traced here: 26.4 us
  Pallas kernels  25.2 us (95%)
  between operations  0.66 us (2%)
  local copies, waits for them, and re-layouts  0.61 us (2%)
    pallas_call x1, Pallas kernels, step(): pl.pallas_call(functools.partial(kernel, groups), out_shape=pltpu.VMEM(co...  25.2 us
    unnamed x1, local copies, waits for them, and re-layouts  0.61 us

profile of v11, /device:TPU:8, one launch (start us, length us, event | category | flops | bytes accessed | tf_op | source)
XLA Modules:
  0.0 26.4 jit_solution(2763278396805798104)
XLA Ops:
  0.7 25.2 %shard_map.64 = bf16[2,16,160]{2,1,0:T(8,128)(2,1)S(1)} custom-call(s32[1]{0:T(128)S(6)} %copy.9.count, s32[512]{0:T(512)} %target_hbm.1, s32[512]{0:T(512)} %source_hbm.1, bf16[2,16,160]{2,1,0:T(8,128)(2,1)} %coeffs_hbm.1, bf16[64,80,160]{2,1,0:T(8,128)(2,1)} %trans_hbm.1, bf16[32,80,160]{2,1,0:T(8,128)(2,1)} %tmat_hbm.1), custom_call_target="tpu_custom_call" | custom-call | tf_op jit(solution)/shard_map/pallas_call | solution.py:336
  25.8 0.6 %copy.8 = bf16[2,16,160]{2,1,0:T(8,128)(2,1)} copy(bf16[2,16,160]{2,1,0:T(8,128)(2,1)S(1)} %shard_map.64) | data formatting | bytes 20480
